TPU v7x, 256 devices: a whole 4x4x8 slice. The times are simulated.
256 devices in a mesh: wide: 32 (over z, y_hi, core), narrow: 8 (over x, y_lo).
Axes of the slice: x: 4, y: 4 (y_hi: 2, y_lo: 2; y = y_hi * 2 + y_lo), z: 8, core: 2. Of those that a mesh axis runs over, the one named last changes fastest.
Arguments:
- hidden: bfloat16 [65536, 8192], P(('wide', 'narrow')), may hold values from -24 to 24
- key_grad: bfloat16 [65536, 512], P(('wide', 'narrow')), may hold values from -6 to 6
- positions: int32 [65536], P(('wide', 'narrow')), may hold values from 0 to 4095
- weight_codes: bfloat16 [8192, 512], P('narrow'), may hold values from -127 to 127
- weight_scales: bfloat16 [8192, 2], P('narrow'), may hold values from 9.9658966e-05 to 0.0009994507
- master: float32 [8192, 512], P(('narrow', 'wide')), may hold values from -0.0625 to 0.0625
- moment: float32 [8192, 512], P(('narrow', 'wide')), may hold values from -6 to 6
- second: float32 [8192, 512], P(('narrow', 'wide')), may hold values from 0.5 to 4
Outputs:
- keys_out: bfloat16 [65536, 512], P(('wide', 'narrow'))
- hidden_grad: bfloat16 [65536, 8192], P(('wide', 'narrow'))
- gradient: float32 [8192, 512], P(('narrow', 'wide'))
- master_out: float32 [8192, 512], P(('narrow', 'wide'))
- moment_out: float32 [8192, 512], P(('narrow', 'wide'))
- second_out: float32 [8192, 512], P(('narrow', 'wide'))
- new_codes: bfloat16 [8192, 512], P('narrow')
- new_scales: bfloat16 [8192, 2], P('narrow')
All inputs are finite; a program needn't handle non-finite values.
Results may differ from a plain program's by a relative error of at most 0.025.
Values may be sent and summed in bfloat16 or wider, within the bound.
A program may use at most 128 MiB of HBM per device.

v0:
```python
import jax
import jax.numpy as jnp
from jax import lax
from jax.sharding import PartitionSpec as P

HEAD = 128
BLOCK = 256


ROPE_BASE = 1000000.0
LEARN_RATE = 0.002
FIRST_DECAY = 0.9
SECOND_DECAY = 0.95
FIRST_FIX = 0.9999734386011124
SECOND_FIX = 0.994079470779666
ADAM_EPSILON = 1e-08
SCALE_EPSILON = 1e-06
CODE_RANGE = 127.0


def split_up(array, dim, devices):
    before, after = (array.shape[:dim], array.shape[dim + 1 :])
    return jnp.moveaxis(array.reshape(*before, devices, -1, *after), dim, 0)


def sum_at_owner(array, axis, dim):
    tiles = split_up(array, dim, lax.axis_size(axis))
    arrived = lax.all_to_all(tiles, axis, split_axis=0, concat_axis=0, tiled=True)
    return arrived.astype(jnp.float32).sum(axis=0)


def from_everyone(array, axis):
    copies = jnp.broadcast_to(array, (lax.axis_size(axis), *array.shape))
    return lax.all_to_all(copies, axis, split_axis=0, concat_axis=0, tiled=True)


def joined_along(tiles, dim):
    dims = list(tiles.shape[1:])
    dims[dim] *= tiles.shape[0]
    return jnp.moveaxis(tiles, 0, dim).reshape(dims)


def gather_directly(array, axis, dim):
    tiles = from_everyone(array, axis)
    return joined_along(tiles, dim)


def in_one_piece(arrays, axis, dim, along):
    both = jnp.concatenate(arrays, axis=along)
    out, at, finished = (lax.all_gather(both, axis, axis=dim, tiled=True), 0, [])
    for a in arrays:
        finished.append(lax.slice_in_dim(out, at, at + a.shape[along], axis=along))
        at += a.shape[along]
    return tuple(finished)


def dequantize(weight_codes, weight_scales):
    height, width = weight_codes.shape
    blocks = weight_scales.shape[1]
    grouped = weight_codes.astype(jnp.float32).reshape(height, blocks, width // blocks)
    grouped = grouped * weight_scales.astype(jnp.float32)[:, :, None]
    return grouped.reshape(height, width).astype(jnp.bfloat16)


def rotation(positions, head_size):
    half_size = head_size // 2
    powers = jnp.arange(half_size, dtype=jnp.float32) * (-2.0 / head_size)
    frequency = jnp.power(jnp.float32(ROPE_BASE), powers)
    angles = positions.astype(jnp.float32)[:, None] * frequency[None, :]
    cosine = jnp.cos(angles)
    sines = jnp.sin(angles)
    return (jnp.concatenate([cosine, cosine], 1), jnp.concatenate([sines, sines], 1))


def turn_half(values):
    half_size = values.shape[-1] // 2
    return jnp.concatenate([-values[..., half_size:], values[..., :half_size]], -1)


def apply_rotation(values, cosine, sines, head_size):
    count, width = values.shape
    heads = values.reshape(count, width // head_size, head_size)
    turned = heads * cosine[:, None, :] + turn_half(heads) * sines[:, None, :]
    return turned.reshape(count, width)


def undo_rotation(values, cosine, sines, head_size):
    count, width = values.shape
    heads = values.reshape(count, width // head_size, head_size)
    scaled = heads * sines[:, None, :]
    reverted = heads * cosine[:, None, :] - turn_half(scaled)
    return reverted.reshape(count, width)


def adam_update(gradient, master, moment, second):
    moment_out = FIRST_DECAY * moment + (1.0 - FIRST_DECAY) * gradient
    second_out = SECOND_DECAY * second + (1.0 - SECOND_DECAY) * gradient * gradient
    step_size = moment_out / FIRST_FIX / (jnp.sqrt(second_out / SECOND_FIX) + ADAM_EPSILON)
    master_out = master - LEARN_RATE * step_size
    return (master_out, moment_out, second_out)


def requantize(master_out, block_width):
    height, width = master_out.shape
    grouped = master_out.reshape(height, width // block_width, block_width)
    peak = jnp.max(jnp.abs(grouped), axis=2)
    new_scales = ((peak + SCALE_EPSILON) / CODE_RANGE).astype(jnp.bfloat16)
    divisor = lax.optimization_barrier(new_scales).astype(jnp.float32)
    new_codes = (grouped / divisor[:, :, None]).reshape(height, width).astype(jnp.bfloat16)
    return (new_codes, new_scales)


def shards(hidden, key_grad, positions, weight_codes, weight_scales, master, moment, second):
    narrow_count = lax.axis_size("narrow")
    wide_count = lax.axis_size("wide")
    devices_all = narrow_count * wide_count
    token_count = hidden.shape[0]
    cosine, sines = rotation(positions, HEAD)
    back_grad = undo_rotation(key_grad.astype(jnp.float32), cosine, sines, HEAD).astype(
        jnp.bfloat16
    )
    local_weight = dequantize(weight_codes, weight_scales)
    column_rows = lax.all_to_all(hidden, "narrow", split_axis=1, concat_axis=0, tiled=True)
    key_terms = jnp.dot(column_rows, local_weight, preferred_element_type=jnp.float32)
    raw_keys = sum_at_owner(key_terms.astype(jnp.bfloat16), "narrow", 0)
    keys_out = apply_rotation(raw_keys, cosine, sines, HEAD).astype(jnp.bfloat16)
    back_all = gather_directly(back_grad, "narrow", 0)
    column_grad = lax.dot_general(
        back_all, local_weight, (((1,), (1,)), ((), ())), preferred_element_type=jnp.float32
    ).astype(jnp.bfloat16)
    hidden_grad = lax.all_to_all(column_grad, "narrow", split_axis=0, concat_axis=1, tiled=True)
    part_width = column_rows.shape[1]
    partials = lax.dot_general(
        column_rows.reshape(narrow_count, token_count, part_width),
        back_all.reshape(narrow_count, token_count, back_all.shape[1]),
        (((1,), (1,)), ((0,), (0,))),
        preferred_element_type=jnp.float32,
    ).astype(jnp.bfloat16)
    partials = lax.optimization_barrier(partials)
    group_sum = jnp.sum(partials.astype(jnp.float32), axis=0)
    summed = sum_at_owner(group_sum.astype(jnp.bfloat16), "wide", 0)
    gradient = summed / jnp.float32(devices_all)
    master_out, moment_out, second_out = adam_update(gradient, master, moment, second)
    local_codes, local_scales = requantize(master_out, BLOCK)
    new_codes, new_scales = in_one_piece((local_codes, local_scales), "wide", 0, 1)
    return (
        keys_out,
        hidden_grad,
        gradient,
        master_out,
        moment_out,
        second_out,
        new_codes,
        new_scales,
    )


def solution(mesh):
    in_specs = (
        P(("wide", "narrow"), None),
        P(("wide", "narrow"), None),
        P(("wide", "narrow")),
        P("narrow", None),
        P("narrow", None),
        P(("narrow", "wide"), None),
        P(("narrow", "wide"), None),
        P(("narrow", "wide"), None),
    )
    out_specs = (
        P(("wide", "narrow"), None),
        P(("wide", "narrow"), None),
        P(("narrow", "wide"), None),
        P(("narrow", "wide"), None),
        P(("narrow", "wide"), None),
        P(("narrow", "wide"), None),
        P("narrow", None),
        P("narrow", None),
    )
    return jax.shard_map(shards, mesh=mesh, in_specs=in_specs, out_specs=out_specs, check_vma=False)
```

profile of v0, /device:TPU:71, one launch (start us, length us, event | category | flops | bytes accessed | tf_op | source)
XLA Modules:
  0.0 308.0 jit_solution(2255532120274280494)
XLA Ops:
  7.2 6.4 %copy.40 = bf16[256,8192]{0,1:T(8,128)(2,1)} copy(bf16[256,8192]{1,0:T(8,128)(2,1)} %param.8) | data formatting | bytes 8388608 | tf_op args[0]
  13.5 6.5 %copy.41 = bf16[256,8,1024]{2,0,1:T(8,128)(2,1)} copy(bf16[256,8,1024]{0,2,1:T(8,128)(2,1)} %bitcast.44) | data formatting | bytes 8388608 | tf_op jit(solution)/shard_map/all_to_all | solution.py:123
  20.0 5.4 %all-to-all-start = ((bf16[256,8,1024]{2,0,1:T(8,128)(2,1)}), bf16[256,8,1024]{2,0,1:T(8,128)(2,1)}, u32[]{:S(2)}, u32[]{:S(2)}) async-start(bf16[256,8,1024]{2,0,1:T(8,128)(2,1)} %copy.41), calls=%async_computation | async-start | bytes 8388608 | tf_op jit(solution)/shard_map/all_to_all | solution.py:123
  25.3 0.0 copy-done.6
  25.4 0.2 copy.39
  25.5 1.2 mul.103
  26.8 0.0 copy-start.8
  26.8 0.2 copy.53
  27.0 0.0 copy-start
  27.0 55.8 %all-to-all-done = bf16[256,8,1024]{2,0,1:T(8,128)(2,1)} async-done(((bf16[256,8,1024]{2,0,1:T(8,128)(2,1)}), bf16[256,8,1024]{2,0,1:T(8,128)(2,1)}, u32[]{:S(2)}, u32[]{:S(2)}) %all-to-all-start) | async-done | bytes 4194336 | tf_op jit(solution)/shard_map/all_to_all | solution.py:123
  82.8 0.0 copy-done.8
  82.8 4.6 %convolution_convert_fusion.1 = bf16[512,2048]{1,0:T(8,128)(2,1)S(1)} fusion(bf16[2048,1024]{1,0:T(8,128)(2,1)} %bitcast.2, f32[1024,512]{1,0:T(8,128)S(1)} %bitcast.52, bf16[1024,512]{1,0:T(8,128)(2,1)S(1)} %copy-done.8), kind=kOutput, calls=%fused_computation.4 | convolution fusion | flops 2150105088 | bytes 9437184 | tf_op jit(solution)/shard_map/dot_general | solution.py:124
  87.4 0.0 copy-done
  87.4 1.5 copy.56
  88.9 5.2 %all-to-all-start.1 = ((bf16[8,256,512]{1,2,0:T(8,128)(2,1)}), bf16[8,256,512]{1,2,0:T(8,128)(2,1)S(1)}, u32[]{:S(2)}, u32[]{:S(2)}) async-start(bf16[8,256,512]{1,2,0:T(8,128)(2,1)} %bitcast.46), calls=%async_computation.1 | async-start | bytes 4194304 | tf_op jit(solution)/shard_map/all_to_all | solution.py:28
  94.1 0.1 copy.44
  94.3 0.3 multiply_cosine_fusion
  94.6 25.3 %all-to-all-done.1 = bf16[8,256,512]{1,2,0:T(8,128)(2,1)S(1)} async-done(((bf16[8,256,512]{1,2,0:T(8,128)(2,1)}), bf16[8,256,512]{1,2,0:T(8,128)(2,1)S(1)}, u32[]{:S(2)}, u32[]{:S(2)}) %all-to-all-start.1) | async-done | bytes 2097184 | tf_op jit(solution)/shard_map/all_to_all | solution.py:28
  119.9 0.3 convert_reduce_fusion
  120.2 0.1 broadcast_multiply_fusion
  120.4 0.2 fusion.4
  120.6 0.1 broadcast_in_dim.2
  120.8 29.2 %all_to_all.53 = bf16[8,256,512]{1,2,0:T(8,128)(2,1)S(1)} all-to-all(bf16[8,256,512]{1,2,0:T(8,128)(2,1)S(1)} %broadcast_in_dim.2), channel_id=1, replica_groups=mesh['wide'=32,'narrow'=8] {'narrow'}, dimensions={0} | all-to-all | bytes 4194304 | tf_op jit(solution)/shard_map/all_to_all | solution.py:34
  149.9 7.8 %convert_bitcast_fusion = bf16[8,1024,512]{1,2,0:T(8,128)(2,1)} fusion(bf16[8,256,512]{1,2,0:T(8,128)(2,1)S(1)} %all_to_all.53, bf16[256,8,1024]{2,0,1:T(8,128)(2,1)} %all-to-all-done), kind=kOutput, calls=%fused_computation | convolution fusion | flops 2151677952 | bytes 14680064 | tf_op jit(solution)/shard_map/dot_general | solution.py:133
  157.7 5.7 %reduce_sum.31 = bf16[1024,512]{0,1:T(8,128)(2,1)S(1)} reduce(bf16[8,1024,512]{1,2,0:T(8,128)(2,1)} %convert_bitcast_fusion, bf16[]{:T(256)} %constant.10.clone.1), dimensions={0}, to_apply=%region_1.0 | reduce | flops 3670016 | bytes 9437186 | tf_op jit(solution)/shard_map/reduce_sum | solution.py:140
  163.4 1.3 copy.47
  164.7 13.2 %all-to-all-start.4 = ((bf16[32,32,512]{2,1,0:T(8,128)(2,1)}), bf16[32,32,512]{2,1,0:T(8,128)(2,1)S(1)}, u32[]{:S(2)}, u32[]{:S(2)}) async-start(bf16[32,32,512]{2,1,0:T(8,128)(2,1)} %bitcast.50), calls=%async_computation.4 | async-start | bytes 2097152 | tf_op jit(solution)/shard_map/all_to_all | solution.py:28
  177.8 2.4 copy.45
  180.3 6.9 %convolution_convert_fusion = bf16[2048,1024]{1,0:T(8,128)(2,1)} fusion(bf16[2048,512]{1,0:T(8,128)(2,1)} %bitcast.54, f32[1024,512]{1,0:T(8,128)} %bitcast.53, bf16[1024,512]{1,0:T(8,128)(2,1)} %param.11), kind=kOutput, calls=%fused_computation.3 | convolution fusion | flops 2151153664 | bytes 9437184 | tf_op jit(solution)/shard_map/dot_general | solution.py:128
  187.2 17.0 %all-to-all-done.4 = bf16[32,32,512]{2,1,0:T(8,128)(2,1)S(1)} async-done(((bf16[32,32,512]{2,1,0:T(8,128)(2,1)}), bf16[32,32,512]{2,1,0:T(8,128)(2,1)S(1)}, u32[]{:S(2)}, u32[]{:S(2)}) %all-to-all-start.4) | async-done | bytes 1048608 | tf_op jit(solution)/shard_map/all_to_all | solution.py:28
  204.1 6.4 %all-to-all-start.3 = ((bf16[8,256,1024]{2,1,0:T(8,128)(2,1)}), bf16[8,256,1024]{2,1,0:T(8,128)(2,1)}, u32[]{:S(2)}, u32[]{:S(2)}) async-start(bf16[8,256,1024]{2,1,0:T(8,128)(2,1)} %bitcast.48), calls=%async_computation.3 | async-start | bytes 8388608 | tf_op jit(solution)/shard_map/all_to_all | solution.py:131
  210.6 0.0 all-gather.2.cloned.1.call-start
  210.6 0.2 convert_reduce_fusion.1
  210.8 0.0 copy-done.3
  210.8 0.0 copy-done.4
  210.8 0.0 copy-done.5
  210.8 0.7 fusion.5
  211.5 0.1 reduce_max.9
  211.7 0.1 div.47
  211.8 0.6 pad_maximum_fusion.3
  212.4 0.0 all-gather.2.cloned.1.call-update
  212.4 0.8 copy.48
  213.3 54.7 %all-to-all-done.3 = bf16[8,256,1024]{2,1,0:T(8,128)(2,1)} async-done(((bf16[8,256,1024]{2,1,0:T(8,128)(2,1)}), bf16[8,256,1024]{2,1,0:T(8,128)(2,1)}, u32[]{:S(2)}, u32[]{:S(2)}) %all-to-all-start.3) | async-done | bytes 4194336 | tf_op jit(solution)/shard_map/all_to_all | solution.py:131
  268.0 4.9 %copy.52 = bf16[8,32,8,1024]{3,2,0,1:T(8,128)(2,1)} copy(bf16[8,32,8,1024]{3,2,1,0:T(8,128)(2,1)} %bitcast.17) | data formatting | bytes 8388608 | tf_op jit(solution)/shard_map/all_to_all | solution.py:131
  272.9 24.3 %all-gather.2.cloned.1.call-done = bf16[1024,514]{1,0:T(8,128)(2,1)} async-done(((bf16[32,514]{1,0:T(8,128)(2,1)}), bf16[1024,514]{1,0:T(8,128)(2,1)}) %all-gather.2.cloned.1.call-update) | async-done | bytes 1052688 | tf_op jit(solution)/shard_map/all_gather | solution.py:50
  297.2 1.0 slice.29
  298.2 0.7 copy.49
  298.9 2.3 slice.28
  (21 shorter events, 0.2 us)
Async XLA Ops:
  20.0 5.4 %copy-start.6 = (bf16[1024,2]{0,1:T(2,128)(2,1)S(1)}, bf16[1024,2]{0,1:T(2,128)(2,1)}, u32[]{:S(2)}) copy-start(bf16[1024,2]{0,1:T(2,128)(2,1)} %param.12) | copy-start | bytes 12292
  20.0 62.8 %all-to-all-start = ((bf16[256,8,1024]{2,0,1:T(8,128)(2,1)}), bf16[256,8,1024]{2,0,1:T(8,128)(2,1)}, u32[]{:S(2)}, u32[]{:S(2)}) async-start(bf16[256,8,1024]{2,0,1:T(8,128)(2,1)} %copy.41), calls=%async_computation | async-start | bytes 8388608 | tf_op jit(solution)/shard_map/all_to_all | solution.py:123
  26.8 56.0 %copy-start.8 = (bf16[1024,512]{1,0:T(8,128)(2,1)S(1)}, bf16[1024,512]{1,0:T(8,128)(2,1)}, u32[]{:S(2)}) copy-start(bf16[1024,512]{1,0:T(8,128)(2,1)} %param.11) | copy-start | bytes 3145732
  27.0 60.4 %copy-start = (f32[128,8,2,256]{3,1,2,0:T(8,128)}, f32[128,8,2,256]{3,1,2,0:T(8,128)S(1)}, u32[]{:S(2)}) copy-start(f32[128,8,2,256]{3,1,2,0:T(8,128)S(1)} %copy.53) | copy-start | bytes 6291460
  88.9 5.2 %copy-start.7 = (s32[256]{0:T(256)S(1)}, s32[256]{0:T(256)}, u32[]{:S(2)}) copy-start(s32[256]{0:T(256)} %param.10) | copy-start | bytes 3076
  88.9 5.2 %copy-start.2 = (bf16[256,512]{1,0:T(8,128)(2,1)S(1)}, bf16[256,512]{1,0:T(8,128)(2,1)}, u32[]{:S(2)}) copy-start(bf16[256,512]{1,0:T(8,128)(2,1)} %param.9) | copy-start | bytes 786436
  88.9 31.0 %all-to-all-start.1 = ((bf16[8,256,512]{1,2,0:T(8,128)(2,1)}), bf16[8,256,512]{1,2,0:T(8,128)(2,1)S(1)}, u32[]{:S(2)}, u32[]{:S(2)}) async-start(bf16[8,256,512]{1,2,0:T(8,128)(2,1)} %bitcast.46), calls=%async_computation.1 | async-start | bytes 4194304 | tf_op jit(solution)/shard_map/all_to_all | solution.py:28
  164.7 39.5 %all-to-all-start.4 = ((bf16[32,32,512]{2,1,0:T(8,128)(2,1)}), bf16[32,32,512]{2,1,0:T(8,128)(2,1)S(1)}, u32[]{:S(2)}, u32[]{:S(2)}) async-start(bf16[32,32,512]{2,1,0:T(8,128)(2,1)} %bitcast.50), calls=%async_computation.4 | async-start | bytes 2097152 | tf_op jit(solution)/shard_map/all_to_all | solution.py:28
  204.1 6.6 %copy-start.3 = (f32[32,512]{1,0:T(8,128)S(1)}, f32[32,512]{1,0:T(8,128)}, u32[]{:S(2)}) copy-start(f32[32,512]{1,0:T(8,128)} %param.13) | copy-start | bytes 196612
  204.1 6.6 %copy-start.4 = (f32[32,512]{1,0:T(8,128)S(1)}, f32[32,512]{1,0:T(8,128)}, u32[]{:S(2)}) copy-start(f32[32,512]{1,0:T(8,128)} %param.14) | copy-start | bytes 196612
  204.1 6.6 %copy-start.5 = (f32[32,512]{1,0:T(8,128)S(1)}, f32[32,512]{1,0:T(8,128)}, u32[]{:S(2)}) copy-start(f32[32,512]{1,0:T(8,128)} %param.15) | copy-start | bytes 196612
  204.1 63.8 %all-to-all-start.3 = ((bf16[8,256,1024]{2,1,0:T(8,128)(2,1)}), bf16[8,256,1024]{2,1,0:T(8,128)(2,1)}, u32[]{:S(2)}, u32[]{:S(2)}) async-start(bf16[8,256,1024]{2,1,0:T(8,128)(2,1)} %bitcast.48), calls=%async_computation.3 | async-start | bytes 8388608 | tf_op jit(solution)/shard_map/all_to_all | solution.py:131
  210.6 86.6 %all-gather.2.cloned.1.call-start = ((), (), s32[]{:S(2)}) async-start(), calls=%async_computation.5 | async-start | bytes 1351680 | tf_op jit(solution)/shard_map/all_gather | solution.py:50
  211.5 61.4 %copy-start.1 = (f32[32,512]{1,0:T(8,128)}, f32[32,512]{1,0:T(8,128)S(1)}, u32[]{:S(2)}) copy-start(f32[32,512]{1,0:T(8,128)S(1)} %get-tuple-element.41) | copy-start | bytes 196612
Sparse Core Ops, SparseCore 0:
  214.7 82.4 all-gather.1
where the time goes:
time: 311 us; the launch traced here: 308 us
  waiting for transfers between devices  177 us (57%)
  starting transfers between devices  30.2 us (10%)
  local copies, waits for them, and re-layouts  29.8 us (10%)
  blocking collectives  29.2 us (9%)
  matrix products  19.2 us (6%)
  between operations  14.3 us (5%)
  other arithmetic  8.27 us (3%)
    all_to_all x1, waiting for transfers between devices, shards(): lax.all_to_all(hidden, 'narrow', split_axis=1, concat_axis=0, tiled=True)  55.8 us
    all_to_all x1, waiting for transfers between devices, shards(): lax.all_to_all(column_grad, 'narrow', split_axis=0, concat_axis=1, tiled=...  54.7 us
    all_to_all x2, waiting for transfers between devices, sum_at_owner(): lax.all_to_all(tiles, axis, split_axis=0, concat_axis=0, tiled=True)  42.3 us
    all_to_all x1, blocking collectives, from_everyone(): return lax.all_to_all(copies, axis, split_axis=0, concat_axis=0, tiled=True)  29.2 us
    all_gather x1, waiting for transfers between devices, in_one_piece(): lax.all_gather(both, axis, axis=dim, tiled=True)  24.3 us
    all_to_all x2, starting transfers between devices, sum_at_owner(): lax.all_to_all(tiles, axis, split_axis=0, concat_axis=0, tiled=True)  18.4 us
    unnamed x24, local copies, waits for them, and re-layouts  8.3 us
    dot_general x1, matrix products, shards(): lax.dot_general(column_rows.reshape(narrow_count, token_count, part_width...  7.76 us
  transfers between devices with their start and end apart: 5, of which 5 were waited for; matrix products, arithmetic and copies ran while one was open for 6% of the time, Pallas kernels for 0%

commit v1 on v0

v1 whole, which is shorter than its diff:
```python
import jax
import jax.numpy as jnp
from jax import lax
from jax.experimental import pallas as pl
from jax.experimental.pallas import tpu as pltpu
from jax.sharding import PartitionSpec as P

HEAD = 128
ROPE_BASE = 1000000.0
LEARN_RATE = 0.002
FIRST_DECAY = 0.9
SECOND_DECAY = 0.95
FIRST_FIX = 0.9999734386011124
SECOND_FIX = 0.994079470779666
ADAM_EPSILON = 1e-08
SCALE_EPSILON = 1e-06
CODE_RANGE = 127.0

MESH = pl.DeviceIdType.MESH
F32 = jnp.float32
BF16 = jnp.bfloat16
ZN = 8
STEPS = ZN - 1
LAG = 3


def device(z, y, x, core):
    return (z * 4 + lax.div(y, 2) * 2 + core, x * 2 + lax.rem(y, 2))


def dot_rows(a, b):
    return lax.dot_general(a, b, (((0,), (0,)), ((), ())), preferred_element_type=F32)


def exchange_kernel(
    hid_hbm, key_grad, cosine, sines, codes, scales, master, moment, second,
    w_hbm, back_out, keys_out, grad_out, master_out, moment_out, second_out, cg_hbm,
    hid, hidp, backp, wg, pbuf, sendbuf, recvbuf, zsum, a2a, cg, acc,
    hid_sem, w_sem, cg_sem, hsend, hrecv, bsend, brecv, wsend, wrecv,
    zsend, zrecv, asend, arecv, gsend, grecv, dsend, drecv,
):
    wide = lax.axis_index("wide")
    narrow = lax.axis_index("narrow")
    z, yh, c = lax.div(wide, 4), lax.rem(lax.div(wide, 2), 2), lax.rem(wide, 2)
    x, yl = lax.div(narrow, 2), lax.rem(narrow, 2)
    y = yh * 2 + yl
    oc = 1 - c
    partner = device(z, y, x, oc)
    xs = {d: lax.rem(x + d + 4, 4) for d in (-1, 1, 2)}
    xs[0] = x
    ys = {d: lax.rem(y + d + 4, 4) for d in (-1, 1)}

    load = pltpu.make_async_copy(hid_hbm, hid, hid_sem)
    load.start()

    def send_hidden(xd):
        cols = pl.ds(pl.multiple_of((xd * 2 + oc) * 1024, 1024), 1024)
        return pltpu.make_async_remote_copy(
            hid_hbm.at[:, cols], hidp.at[xd], hsend, hrecv.at[xd], partner, MESH
        )

    for xd in range(4):
        send_hidden(xd).start()

    lane = lax.broadcasted_iota(jnp.int32, (256, HEAD), 1)
    cos = cosine[...]
    sin = jnp.where(lane < HEAD // 2, -sines[...], sines[...])
    for h in range(4):
        s = slice(h * HEAD, (h + 1) * HEAD)
        v = key_grad[:, s].astype(F32)
        back_out[:, s] = (v * cos - pltpu.roll(v, HEAD // 2, 1) * sin).astype(BF16)
    send_back = pltpu.make_async_remote_copy(back_out, backp, bsend, brecv, partner, MESH)
    send_back.start()

    pick = (
        lax.broadcasted_iota(jnp.int32, (2, 512), 1) // 256
        == lax.broadcasted_iota(jnp.int32, (2, 512), 0)
    ).astype(BF16)

    @pl.loop(0, 8)
    def _(i):
        rows = pl.ds(pl.multiple_of(i * 128, 128), 128)
        factor = dot_rows(scales[:, rows], pick)
        wg[narrow, rows, :] = (codes[rows, :].astype(F32) * factor).astype(BF16)

    def chunk(xb, lo, half, q):
        return wg.at[xb * 2 + lo, pl.ds(pl.multiple_of(half * 512 + q * 256, 256), 256)]

    def w_copy(xb, lo, half, q, target):
        ref = chunk(xb, lo, half, q)
        sem = wrecv.at[xb * 2 + lo, half, q]
        return pltpu.make_async_remote_copy(ref, ref, wsend, sem, target, MESH)

    def w_wait(xb, lo, half, q):
        w_copy(xb, lo, half, q, partner).wait_recv()

    def to_x(xb, q, d):
        w_copy(xb, yl, c, q, device(z, y, xs[d], c)).start()

    def to_y(xb, q):
        w_copy(xb, yl, c, q, device(z, ys[1 - 2 * q], x, c)).start()

    def to_partner(xb, lo, q):
        w_copy(xb, lo, c, q, partner).start()

    for q in range(2):
        to_x(x, q, 1)
        to_x(x, q, -1)
        to_y(x, q)

    load.wait()

    def keys_of(xb, lo, first=False):
        block = xb * 2 + lo
        if not first:
            w_wait(xb, lo, oc, 0)
            w_wait(xb, lo, oc, 1)
        pltpu.make_async_copy(wg.at[block], w_hbm.at[block], w_sem).start()
        cols = pl.ds(pl.multiple_of(block * 1024, 1024), 1024)
        term = jnp.dot(hid[:, cols], wg[block], preferred_element_type=F32)
        acc[...] = term if first else acc[...] + term

    def partials(p, step):
        for xd in range(4):
            way = 1 if xd < 2 else -1
            at = lax.rem(z - way * (step + 1) + 2 * ZN, ZN)
            own = pl.ds(pl.multiple_of((xd * 2 + c) * 1024 + at * 128, 128), 128)
            other = pl.ds(pl.multiple_of(at * 128, 128), 128)
            cols = slice(p * 256, (p + 1) * 256)
            pbuf[p, xd] = dot_rows(hid[:, own], back_out[:, cols]) + dot_rows(
                hidp[xd, :, other], backp[:, cols]
            )

    def z_copy(p, xd, step):
        way = 1 if xd < 2 else -1
        to = device(lax.rem(z + way + ZN, ZN), y, x, c)
        return pltpu.make_async_remote_copy(
            sendbuf.at[p, xd, step], recvbuf.at[p, xd, step],
            zsend, zrecv.at[p, xd, step], to, MESH,
        )

    def z_step(p, step):
        for xd in range(4):
            @pl.when(step > 0)
            def _():
                z_copy(p, xd, step - 1).wait_recv()
                pbuf[p, xd] += recvbuf[p, xd, step - 1].astype(F32)

            sendbuf[p, xd, step] = pbuf[p, xd].astype(BF16)
            z_copy(p, xd, step).start()
        partials(p, step + 1)

    def plane_copy(p, i):
        xd, yhd, cd = lax.div(i, 4), lax.rem(lax.div(i, 2), 2), lax.rem(i, 2)
        rows = pl.ds(pl.multiple_of(yhd * 64 + cd * 32, 32), 32)
        src, dst = zsum.at[p, xd, rows], a2a.at[p, x * 4 + y]
        mine = (xd == x) & (yl == c) & (yhd == yh) & (cd == c)
        remote = pltpu.make_async_remote_copy(
            src, dst, asend.at[p], arecv.at[p], device(z, yhd * 2 + c, xd, cd), MESH
        )
        return mine, remote, pltpu.make_async_copy(src, dst, arecv.at[p])

    def to_plane(p):
        for xd in range(4):
            z_copy(p, xd, STEPS - 1).wait_recv()
            zsum[p, xd] = (pbuf[p, xd] + recvbuf[p, xd, STEPS - 1].astype(F32)).astype(BF16)

        @pl.loop(0, 16)
        def _(i):
            mine, remote, local = plane_copy(p, i)

            @pl.when(mine)
            def _():
                local.start()

            @pl.when(jnp.logical_not(mine))
            def _():
                remote.start()

    def span(p):
        return slice(0, 256) if p == 0 else slice(256, 640)

    def code_copy(p, i):
        zd, yhd = lax.div(i, 2), lax.rem(i, 2)
        ref = cg.at[z, yh, c, :, span(p)]
        mine = (zd == z) & (yhd == yh)
        return mine, pltpu.make_async_remote_copy(
            ref, ref, gsend.at[p], grecv.at[p], device(zd, yhd * 2 + yl, x, c), MESH
        )

    def update(p):
        pltpu.make_async_copy(a2a.at[p], a2a.at[p], arecv.at[p]).wait()
        total = a2a[p, 0].astype(F32)
        for i in range(1, 16):
            total = total + a2a[p, i].astype(F32)
        cols = slice(p * 256, (p + 1) * 256)
        gradient = total / 256.0
        moment_new = FIRST_DECAY * moment[:, cols] + (1.0 - FIRST_DECAY) * gradient
        second_new = SECOND_DECAY * second[:, cols] + (1.0 - SECOND_DECAY) * gradient * gradient
        step_size = moment_new / FIRST_FIX / (jnp.sqrt(second_new / SECOND_FIX) + ADAM_EPSILON)
        master_new = master[:, cols] - LEARN_RATE * step_size
        grad_out[:, cols] = gradient
        moment_out[:, cols] = moment_new
        second_out[:, cols] = second_new
        master_out[:, cols] = master_new
        peak = jnp.max(jnp.abs(master_new), axis=1, keepdims=True)
        scale = ((peak + SCALE_EPSILON) / CODE_RANGE).astype(BF16).astype(F32)
        cg[z, yh, c, :, cols] = (master_new / scale).astype(BF16)
        spread = jnp.broadcast_to(scale, (32, HEAD))
        if p == 1:
            at = lax.broadcasted_iota(jnp.int32, (32, HEAD), 1)
            spread = jnp.where(at == 0, cg[z, yh, c, :, 512:640].astype(F32), spread)
        cg[z, yh, c, :, 512:640] = spread.astype(BF16)

        @pl.loop(0, 16)
        def _(i):
            mine, remote = code_copy(p, i)

            @pl.when(jnp.logical_not(mine))
            def _():
                remote.start()

    def fifteen(p, sem):
        same = a2a.at[0, pl.ds(0, 15)] if p == 0 else hid.at[0:32, 0 : 15 * 384]
        pltpu.make_async_copy(same, same, sem).wait()

    def pass_copy(p):
        ref = cg.at[:, :, c, :, span(p)]
        return pltpu.make_async_remote_copy(
            ref, ref, dsend.at[p], drecv.at[p], partner, MESH
        )

    for xd in range(4):
        send_hidden(xd).wait_recv()
    send_back.wait_recv()
    partials(0, 0)

    @pl.loop(0, STEPS + LAG)
    def _(t):
        @pl.when(t < STEPS)
        def _():
            z_step(0, t)

        @pl.when(t == LAG - 1)
        def _():
            partials(1, 0)
            keys_of(x, yl, True)

        @pl.when(t >= LAG)
        def _():
            z_step(1, t - LAG)

        @pl.when(t == 2)
        def _():
            w_wait(xs[-1], yl, c, 0)
            to_x(xs[-1], 0, 1)
            to_y(xs[-1], 0)
            to_partner(xs[-1], yl, 0)
            w_wait(xs[1], yl, c, 0)
            to_y(xs[1], 0)
            to_partner(xs[1], yl, 0)
            for q in range(2):
                w_wait(x, 1 - yl, c, q)
                to_partner(x, 1 - yl, q)

        @pl.when(t == 3)
        def _():
            w_wait(xs[1], yl, c, 1)
            to_x(xs[1], 1, -1)
            to_y(xs[1], 1)
            to_partner(xs[1], yl, 1)
            w_wait(xs[-1], yl, c, 1)
            to_y(xs[-1], 1)
            to_partner(xs[-1], yl, 1)
            keys_of(x, 1 - yl)

        @pl.when(t == 4)
        def _():
            for q in range(2):
                w_wait(xs[2], yl, c, q)
                to_y(xs[2], q)
                to_partner(xs[2], yl, q)
            for d in (-1, 1):
                w_wait(xs[d], 1 - yl, c, 0)
                to_partner(xs[d], 1 - yl, 0)
            for d in (-1, 1):
                keys_of(xs[d], yl)

        @pl.when(t == 5)
        def _():
            for d in (-1, 1):
                w_wait(xs[d], 1 - yl, c, 1)
                to_partner(xs[d], 1 - yl, 1)
            keys_of(xs[2], yl)

        @pl.when(t == 6)
        def _():
            for q in range(2):
                w_wait(xs[2], 1 - yl, c, q)
                to_partner(xs[2], 1 - yl, q)
            for d in (-1, 1):
                keys_of(xs[d], 1 - yl)
            to_plane(0)

        @pl.when(t == 7)
        def _():
            keys_of(xs[2], 1 - yl)

        @pl.when(t == 8)
        def _():
            update(0)

    to_plane(1)
    for h in range(4):
        s = slice(h * HEAD, (h + 1) * HEAD)
        v = acc[:, s]
        keys_out[:, s] = (v * cos + pltpu.roll(v, HEAD // 2, 1) * sin).astype(BF16)
    fifteen(0, grecv.at[0])
    pass_copy(0).start()
    update(1)
    fifteen(1, grecv.at[1])
    pass_copy(1).start()

    pltpu.make_async_copy(hidp, hidp, hsend).wait()
    send_back.wait_send()
    pltpu.make_async_copy(wg.at[pl.ds(0, 7)], wg.at[pl.ds(0, 7)], wsend).wait()
    pltpu.make_async_copy(sendbuf, sendbuf, zsend).wait()
    for p in range(2):
        @pl.when(yl == c)
        def _():
            part = a2a.at[p, pl.ds(0, 15)]
            pltpu.make_async_copy(part, part, asend.at[p]).wait()

        @pl.when(yl != c)
        def _():
            pltpu.make_async_copy(a2a.at[p], a2a.at[p], asend.at[p]).wait()

        fifteen(p, gsend.at[p])
        pass_copy(p).wait()
    pltpu.make_async_copy(wg, w_hbm, w_sem).wait()
    last = pltpu.make_async_copy(cg, cg_hbm, cg_sem)
    last.start()
    last.wait()


def exchange(hidden, key_grad, cosine, sines, codes, scales, master, moment, second):
    vmem = pl.BlockSpec(memory_space=pltpu.VMEM)
    anywhere = pl.BlockSpec(memory_space=pl.ANY)
    dma = pltpu.SemaphoreType.DMA
    state = jax.ShapeDtypeStruct((32, 512), F32)
    return pl.pallas_call(
        exchange_kernel,
        out_shape=(
            jax.ShapeDtypeStruct((8, 1024, 512), BF16),
            jax.ShapeDtypeStruct((256, 512), BF16),
            jax.ShapeDtypeStruct((256, 512), BF16),
            state, state, state, state,
            jax.ShapeDtypeStruct((8, 2, 2, 32, 640), BF16),
        ),
        in_specs=[anywhere] + [vmem] * 8,
        out_specs=(anywhere,) + (vmem,) * 6 + (anywhere,),
        scratch_shapes=[
            pltpu.VMEM((256, 8192), BF16),
            pltpu.VMEM((4, 256, 1024), BF16),
            pltpu.VMEM((256, 512), BF16),
            pltpu.VMEM((8, 1024, 512), BF16),
            pltpu.VMEM((2, 4, 128, 256), F32),
            pltpu.VMEM((2, 4, STEPS, 128, 256), BF16),
            pltpu.VMEM((2, 4, STEPS, 128, 256), BF16),
            pltpu.VMEM((2, 4, 128, 256), BF16),
            pltpu.VMEM((2, 16, 32, 256), BF16),
            pltpu.VMEM((8, 2, 2, 32, 640), BF16),
            pltpu.VMEM((256, 512), F32),
            dma, dma, dma,
            dma, dma((4,)), dma, dma, dma, dma((8, 2, 2)),
            dma, dma((2, 4, STEPS)),
            dma((2,)), dma((2,)), dma((2,)), dma((2,)), dma((2,)), dma((2,)),
        ],
        compiler_params=pltpu.CompilerParams(
            has_side_effects=True, vmem_limit_bytes=60 * 1024 * 1024
        ),
    )(hidden, key_grad, cosine, sines, codes, scales, master, moment, second)


def finish_kernel(
    w, back, keys, grad, master, moment, second, cg,
    hidden_grad, keys_out, grad_out, master_out, moment_out, second_out, codes_out, scales_out,
):
    hidden_grad[...] = lax.dot_general(
        back[...], w[0], (((1,), (1,)), ((), ())), preferred_element_type=F32
    ).astype(BF16)

    @pl.when(pl.program_id(0) == 0)
    def _():
        keys_out[...] = keys[...]
        grad_out[...] = grad[...]
        master_out[...] = master[...]
        moment_out[...] = moment[...]
        second_out[...] = second[...]
        codes_out[...] = cg[:, 0:512]
        scales_out[...] = cg[:, 512:640].astype(F32).T[0:2, :].astype(BF16)


def finish(w, back, keys, grad, master, moment, second, cg):
    def whole(*shape):
        return pl.BlockSpec(shape, lambda i: (0,) * len(shape))

    state = jax.ShapeDtypeStruct((32, 512), F32)
    return pl.pallas_call(
        finish_kernel,
        grid=(8,),
        out_shape=(
            jax.ShapeDtypeStruct((256, 8192), BF16),
            jax.ShapeDtypeStruct((256, 512), BF16),
            state, state, state, state,
            jax.ShapeDtypeStruct((1024, 512), BF16),
            jax.ShapeDtypeStruct((2, 1024), BF16),
        ),
        in_specs=[
            pl.BlockSpec((1, 1024, 512), lambda i: (i, 0, 0)),
            whole(256, 512), whole(256, 512),
            whole(32, 512), whole(32, 512), whole(32, 512), whole(32, 512),
            whole(1024, 640),
        ],
        out_specs=(
            pl.BlockSpec((256, 1024), lambda i: (0, i)),
            whole(256, 512),
            whole(32, 512), whole(32, 512), whole(32, 512), whole(32, 512),
            whole(1024, 512), whole(2, 1024),
        ),
    )(w, back, keys, grad, master, moment, second, cg)


def rotation(positions):
    half_size = HEAD // 2
    powers = jnp.arange(half_size, dtype=F32) * (-2.0 / HEAD)
    frequency = jnp.power(F32(ROPE_BASE), powers)
    both = jnp.concatenate([frequency, frequency])
    angles = positions.astype(F32)[:, None] * both[None, :]
    return jnp.cos(angles), jnp.sin(angles)


def shards(hidden, key_grad, positions, weight_codes, weight_scales, master, moment, second):
    cosine, sines = rotation(positions)
    w, back, keys, grad, master_out, moment_out, second_out, cg = exchange(
        hidden, key_grad, cosine, sines, weight_codes, weight_scales.T, master, moment, second
    )
    hidden_grad, keys, grad, master_out, moment_out, second_out, codes, scales = finish(
        w, back, keys, grad, master_out, moment_out, second_out, cg.reshape(1024, 640)
    )
    return (keys, hidden_grad, grad, master_out, moment_out, second_out, codes, scales.T)


def solution(mesh):
    in_specs = (
        P(("wide", "narrow"), None),
        P(("wide", "narrow"), None),
        P(("wide", "narrow")),
        P("narrow", None),
        P("narrow", None),
        P(("narrow", "wide"), None),
        P(("narrow", "wide"), None),
        P(("narrow", "wide"), None),
    )
    out_specs = (
        P(("wide", "narrow"), None),
        P(("wide", "narrow"), None),
        P(("narrow", "wide"), None),
        P(("narrow", "wide"), None),
        P(("narrow", "wide"), None),
        P(("narrow", "wide"), None),
        P("narrow", None),
        P("narrow", None),
    )
    return jax.shard_map(shards, mesh=mesh, in_specs=in_specs, out_specs=out_specs, check_vma=False)
```

time: 311 us -> 114 us (0.37)
  waiting for transfers between devices: 177 us -> 0 us
  Pallas kernels: 0 us -> 109 us
  starting transfers between devices: 30.2 us -> 0 us
  local copies, waits for them, and re-layouts: 29.8 us -> 0 us
  blocking collectives: 29.2 us -> 0 us
  matrix products: 19.2 us -> 0 us
  between operations: 14.3 us -> 0.65 us
  other arithmetic: 8.27 us -> 2.01 us
    all_to_all x4 -> x0, waiting for transfers between devices: 153 us -> none  [the longest x1 55.8 us: shards(): lax.all_to_all(hidden, 'narrow', split_axis=1, concat_axis=0, tiled=True)]
    pallas_call x0 -> x2, Pallas kernels: none -> 109 us  [the longest x1 99.1 us: exchange(): pl.pallas_call(exchange_kernel, out_shape=(jax.ShapeDtypeStruct((8, 1024,...]
    all_to_all x4 -> x0, starting transfers between devices: 30.2 us -> none  [the longest x2 18.4 us: sum_at_owner(): lax.all_to_all(tiles, axis, split_axis=0, concat_axis=0, tiled=True)]
    all_to_all x1 -> x0, blocking collectives: 29.2 us -> none  [from_everyone(): return lax.all_to_all(copies, axis, split_axis=0, concat_axis=0, tiled=True)]
    all_gather x1 -> x0, waiting for transfers between devices: 24.3 us -> none  [in_one_piece(): lax.all_gather(both, axis, axis=dim, tiled=True)]
    dot_general x3 -> x0, matrix products: 19.2 us -> none  [the longest x1 7.76 us: shards(): lax.dot_general(column_rows.reshape(narrow_count, token_count, part_width...]
    all_to_all x3 -> x0, local copies, waits for them, and re-layouts: 13.8 us -> none  [the longest x1 6.45 us: shards(): lax.all_to_all(hidden, 'narrow', split_axis=1, concat_axis=0, tiled=True)]
    unnamed x24 -> x0, local copies, waits for them, and re-layouts: 8.3 us -> none
  transfers between devices with their start and end apart: 5 -> 0, of which waited for: 5 -> 0; matrix products, arithmetic and copies ran while one was open for 6% -> 0% of each run, Pallas kernels for 0% -> 0%
where the time goes in v1:
time: 114 us; the launch traced here: 112 us
  Pallas kernels  109 us (96%)
  other arithmetic  2.01 us (2%)
    pallas_call x1, Pallas kernels, exchange(): pl.pallas_call(exchange_kernel, out_shape=(jax.ShapeDtypeStruct((8, 1024,...  99.1 us
    pallas_call x1, Pallas kernels, finish(): pl.pallas_call(finish_kernel, grid=(8,), out_shape=(jax.ShapeDtypeStruct(...  10.3 us

profile of v1, /device:TPU:71, one launch (start us, length us, event | category | flops | bytes accessed | tf_op | source)
XLA Modules:
  0.0 112.0 jit_solution(13818100377137277305)
XLA Ops:
  0.6 0.1 pad_maximum_fusion
  0.7 0.7 convert_element_type.3
  1.4 1.2 %multiply_sine_fusion = (f32[256,128]{1,0:T(8,128)}, f32[256,128]{1,0:T(8,128)}) fusion(f32[128]{0:T(128)S(1)} %pad_maximum_fusion, f32[256]{0:T(256)S(1)} %convert_element_type.3), kind=kLoop, calls=%fused_computation | loop fusion | flops 32768 | bytes 263680 | tf_op jit(solution)/shard_map/sin | solution.py:440
  2.6 99.1 %shard_map.143 = (bf16[8,1024,512]{2,1,0:T(8,128)(2,1)}, bf16[256,512]{1,0:T(8,128)(2,1)}, bf16[256,512]{1,0:T(8,128)(2,1)}, f32[32,512]{1,0:T(8,128)}, f32[32,5...) custom-call(bf16[256,8192]{1,0:T(8,128)(2,1)} %hid_hbm.1, ...), custom_call_target="tpu_custom_call" | custom-call | tf_op jit(solution)/shard_map/pallas_call | solution.py:351
  101.7 10.3 %shard_map.144 = (bf16[256,8192]{1,0:T(8,128)(2,1)}, bf16[256,512]{1,0:T(8,128)(2,1)}, f32[32,512]{1,0:T(8,128)}, f32[32,512]{1,0:T(8,128)}, f32[32,512]{1,0:T(8...) custom-call(bf16[8,1024,512]{2,1,0:T(8,128)(2,1)} %get-tuple-element.24.w, ...), custom_call_target="tpu_custom_call" | custom-call | tf_op jit(solution)/shard_map/pallas_call | solution.py:409
  (1 shorter events, 0.0 us)

commit v2 on v1

--- a/solution.py
+++ b/solution.py
@@ -33,12 +33,17 @@
 
 
 def exchange_kernel(
-    hid_hbm, key_grad, cosine, sines, codes, scales, master, moment, second,
-    w_hbm, back_out, keys_out, grad_out, master_out, moment_out, second_out, cg_hbm,
-    hid, hidp, backp, wg, pbuf, sendbuf, recvbuf, zsum, a2a, cg, acc,
-    hid_sem, w_sem, cg_sem, hsend, hrecv, bsend, brecv, wsend, wrecv,
-    zsend, zrecv, asend, arecv, gsend, grecv, dsend, drecv,
+    hid_hbm, key_grad_hbm, positions, frequency, codes_hbm, scales, master_hbm, moment_hbm,
+    second_hbm,
+    hg_hbm, keys_hbm, grad_hbm, master_out_hbm, moment_out_hbm, second_out_hbm, cg_hbm,
+    hid, hidp, back_out, backp, wg, hg, pbuf, sendbuf, recvbuf, zsum, a2a, cg, acc,
+    key_grad, codes, keys_out, state,
+    in_sem, hg_sem, cg_sem, out_sem, hsend, hrecv, bsend, brecv, wsend, wrecv,
+    zsend, zrecv, asend, arecv, gsend, grecv, ysend, yrecv, dsend, drecv,
 ):
+    master, moment, second, grad_out, master_out, moment_out, second_out = (
+        state.at[i] for i in range(7)
+    )
     wide = lax.axis_index("wide")
     narrow = lax.axis_index("narrow")
     z, yh, c = lax.div(wide, 4), lax.rem(lax.div(wide, 2), 2), lax.rem(wide, 2)
@@ -50,8 +55,32 @@
     xs[0] = x
     ys = {d: lax.rem(y + d + 4, 4) for d in (-1, 1)}
 
-    load = pltpu.make_async_copy(hid_hbm, hid, hid_sem)
-    load.start()
+    loads = [
+        pltpu.make_async_copy(src, dst, in_sem.at[i])
+        for i, (src, dst) in enumerate((
+            (key_grad_hbm, key_grad), (codes_hbm, codes), (hid_hbm, hid),
+            (master_hbm, master), (moment_hbm, moment), (second_hbm, second),
+        ))
+    ]
+    for load in loads:
+        load.start()
+
+    barrier = pltpu.get_barrier_semaphore()
+
+    @pl.loop(0, 32)
+    def _(i):
+        to = device(z, lax.rem(lax.div(i, 2), 4), lax.div(i, 8), lax.rem(i, 2))
+
+        @pl.when((to[0] != wide) | (to[1] != narrow))
+        def _():
+            pl.semaphore_signal(barrier, inc=1, device_id=to, device_id_type=MESH)
+
+    @pl.loop(0, 16)
+    def _(i):
+        @pl.when(lax.div(i, 2) != z)
+        def _():
+            to = device(lax.div(i, 2), lax.rem(i, 2) * 2 + yl, x, c)
+            pl.semaphore_signal(barrier, inc=1, device_id=to, device_id_type=MESH)
 
     def send_hidden(xd):
         cols = pl.ds(pl.multiple_of((xd * 2 + oc) * 1024, 1024), 1024)
@@ -59,23 +88,27 @@
             hid_hbm.at[:, cols], hidp.at[xd], hsend, hrecv.at[xd], partner, MESH
         )
 
-    for xd in range(4):
-        send_hidden(xd).start()
-
+    place = jnp.concatenate(
+        [jnp.broadcast_to(positions[i : i + 1, :].astype(F32), (128, 128)).T for i in range(2)], 0
+    )
+    angle = place * frequency[...]
+    cos = jnp.cos(angle)
+    sin = jnp.sin(angle)
     lane = lax.broadcasted_iota(jnp.int32, (256, HEAD), 1)
-    cos = cosine[...]
-    sin = jnp.where(lane < HEAD // 2, -sines[...], sines[...])
+    sin = jnp.where(lane < HEAD // 2, -sin, sin)
+    loads[0].wait()
     for h in range(4):
         s = slice(h * HEAD, (h + 1) * HEAD)
         v = key_grad[:, s].astype(F32)
         back_out[:, s] = (v * cos - pltpu.roll(v, HEAD // 2, 1) * sin).astype(BF16)
     send_back = pltpu.make_async_remote_copy(back_out, backp, bsend, brecv, partner, MESH)
-    send_back.start()
 
     pick = (
         lax.broadcasted_iota(jnp.int32, (2, 512), 1) // 256
         == lax.broadcasted_iota(jnp.int32, (2, 512), 0)
     ).astype(BF16)
+
+    loads[1].wait()
 
     @pl.loop(0, 8)
     def _(i):
@@ -103,22 +136,40 @@
     def to_partner(xb, lo, q):
         w_copy(xb, lo, c, q, partner).start()
 
+    pl.semaphore_wait(barrier, 45)
+    for xd in range(4):
+        send_hidden(xd).start()
+    send_back.start()
     for q in range(2):
         to_x(x, q, 1)
         to_x(x, q, -1)
         to_y(x, q)
 
-    load.wait()
-
-    def keys_of(xb, lo, first=False):
+    for load in loads[2:]:
+        load.wait()
+
+    def hg_copy(block):
+        cols = pl.ds(pl.multiple_of(block * 1024, 1024), 1024)
+        return pltpu.make_async_copy(hg.at[:, cols], hg_hbm.at[:, cols], hg_sem)
+
+    def use_block(xb, lo, first=False):
         block = xb * 2 + lo
-        if not first:
+        if first:
+            acc[...] = jnp.zeros_like(acc)
+        else:
             w_wait(xb, lo, oc, 0)
             w_wait(xb, lo, oc, 1)
-        pltpu.make_async_copy(wg.at[block], w_hbm.at[block], w_sem).start()
-        cols = pl.ds(pl.multiple_of(block * 1024, 1024), 1024)
-        term = jnp.dot(hid[:, cols], wg[block], preferred_element_type=F32)
-        acc[...] = term if first else acc[...] + term
+
+        @pl.loop(0, 4)
+        def _(i):
+            cols = pl.ds(pl.multiple_of(block * 1024 + i * 256, 256), 256)
+            w = wg[block, pl.ds(pl.multiple_of(i * 256, 256), 256), :]
+            acc[...] += jnp.dot(hid[:, cols], w, preferred_element_type=F32)
+            hg[:, cols] = lax.dot_general(
+                back_out[...], w, (((1,), (1,)), ((), ())), preferred_element_type=F32
+            ).astype(BF16)
+
+        hg_copy(block).start()
 
     def partials(p, step):
         for xd in range(4):
@@ -131,23 +182,26 @@
                 hidp[xd, :, other], backp[:, cols]
             )
 
-    def z_copy(p, xd, step):
+    def z_copy(p, xd, half, step):
         way = 1 if xd < 2 else -1
         to = device(lax.rem(z + way + ZN, ZN), y, x, c)
+        rows = slice(half * 64, half * 64 + 64)
         return pltpu.make_async_remote_copy(
-            sendbuf.at[p, xd, step], recvbuf.at[p, xd, step],
-            zsend, zrecv.at[p, xd, step], to, MESH,
+            sendbuf.at[p, xd, step, rows], recvbuf.at[p, xd, step, rows],
+            zsend, zrecv.at[p, xd, half, step], to, MESH,
         )
 
     def z_step(p, step):
-        for xd in range(4):
-            @pl.when(step > 0)
-            def _():
-                z_copy(p, xd, step - 1).wait_recv()
-                pbuf[p, xd] += recvbuf[p, xd, step - 1].astype(F32)
-
-            sendbuf[p, xd, step] = pbuf[p, xd].astype(BF16)
-            z_copy(p, xd, step).start()
+        for half in range(2):
+            rows = slice(half * 64, half * 64 + 64)
+            for xd in (0, 2, 1, 3):
+                @pl.when(step > 0)
+                def _():
+                    z_copy(p, xd, half, step - 1).wait_recv()
+                    pbuf[p, xd, rows] += recvbuf[p, xd, step - 1, rows].astype(F32)
+
+                sendbuf[p, xd, step, rows] = pbuf[p, xd, rows].astype(BF16)
+                z_copy(p, xd, half, step).start()
         partials(p, step + 1)
 
     def plane_copy(p, i):
@@ -162,7 +216,8 @@
 
     def to_plane(p):
         for xd in range(4):
-            z_copy(p, xd, STEPS - 1).wait_recv()
+            for half in range(2):
+                z_copy(p, xd, half, STEPS - 1).wait_recv()
             zsum[p, xd] = (pbuf[p, xd] + recvbuf[p, xd, STEPS - 1].astype(F32)).astype(BF16)
 
         @pl.loop(0, 16)
@@ -184,9 +239,15 @@
         zd, yhd = lax.div(i, 2), lax.rem(i, 2)
         ref = cg.at[z, yh, c, :, span(p)]
         mine = (zd == z) & (yhd == yh)
-        return mine, pltpu.make_async_remote_copy(
+        skip = mine if p == 1 else mine | (yhd != yh)
+        return skip, pltpu.make_async_remote_copy(
             ref, ref, gsend.at[p], grecv.at[p], device(zd, yhd * 2 + yl, x, c), MESH
         )
+
+    def over_y():
+        ref = cg.at[:, yh, c, :, span(0)]
+        to = device(z, (1 - yh) * 2 + yl, x, c)
+        return pltpu.make_async_remote_copy(ref, ref, ysend, yrecv, to, MESH)
 
     def update(p):
         pltpu.make_async_copy(a2a.at[p], a2a.at[p], arecv.at[p]).wait()
@@ -220,9 +281,13 @@
             def _():
                 remote.start()
 
-    def fifteen(p, sem):
-        same = a2a.at[0, pl.ds(0, 15)] if p == 0 else hid.at[0:32, 0 : 15 * 384]
+    def arrived(p, sem):
+        same = cg.at[pl.ds(0, 7), 0, 0, :, span(0)] if p == 0 else hid.at[0:32, 0 : 15 * 384]
         pltpu.make_async_copy(same, same, sem).wait()
+
+    def put(p, core):
+        ref = cg.at[:, :, core, :, span(p)]
+        return pltpu.make_async_copy(ref, cg_hbm.at[:, :, core, :, span(p)], cg_sem)
 
     def pass_copy(p):
         ref = cg.at[:, :, c, :, span(p)]
@@ -244,11 +309,14 @@
         @pl.when(t == LAG - 1)
         def _():
             partials(1, 0)
-            keys_of(x, yl, True)
 
         @pl.when(t >= LAG)
         def _():
             z_step(1, t - LAG)
+
+        @pl.when(t == 1)
+        def _():
+            use_block(x, yl, True)
 
         @pl.when(t == 2)
         def _():
@@ -272,9 +340,14 @@
             w_wait(xs[-1], yl, c, 1)
             to_y(xs[-1], 1)
             to_partner(xs[-1], yl, 1)
-            keys_of(x, 1 - yl)
+            use_block(x, 1 - yl)
 
         @pl.when(t == 4)
+        def _():
+            for d in (-1, 1):
+                use_block(xs[d], yl)
+
+        @pl.when(t == 5)
         def _():
             for q in range(2):
                 w_wait(xs[2], yl, c, q)
@@ -283,43 +356,52 @@
             for d in (-1, 1):
                 w_wait(xs[d], 1 - yl, c, 0)
                 to_partner(xs[d], 1 - yl, 0)
-            for d in (-1, 1):
-                keys_of(xs[d], yl)
-
-        @pl.when(t == 5)
-        def _():
+
+        @pl.when(t == 6)
+        def _():
+            to_plane(0)
             for d in (-1, 1):
                 w_wait(xs[d], 1 - yl, c, 1)
                 to_partner(xs[d], 1 - yl, 1)
-            keys_of(xs[2], yl)
-
-        @pl.when(t == 6)
-        def _():
+            use_block(xs[2], yl)
+
+        @pl.when(t == 7)
+        def _():
+            for d in (-1, 1):
+                use_block(xs[d], 1 - yl)
+
+        @pl.when(t == 8)
+        def _():
+            update(0)
             for q in range(2):
                 w_wait(xs[2], 1 - yl, c, q)
                 to_partner(xs[2], 1 - yl, q)
-            for d in (-1, 1):
-                keys_of(xs[d], 1 - yl)
-            to_plane(0)
-
-        @pl.when(t == 7)
-        def _():
-            keys_of(xs[2], 1 - yl)
-
-        @pl.when(t == 8)
-        def _():
-            update(0)
 
     to_plane(1)
+    arrived(0, grecv.at[0])
+    over_y().start()
+    use_block(xs[2], 1 - yl)
     for h in range(4):
         s = slice(h * HEAD, (h + 1) * HEAD)
         v = acc[:, s]
         keys_out[:, s] = (v * cos + pltpu.roll(v, HEAD // 2, 1) * sin).astype(BF16)
-    fifteen(0, grecv.at[0])
+    outs = [pltpu.make_async_copy(keys_out, keys_hbm, out_sem.at[0])]
+    outs[0].start()
+    update(1)
+    for i, (src, dst) in enumerate((
+        (grad_out, grad_hbm), (master_out, master_out_hbm),
+        (moment_out, moment_out_hbm), (second_out, second_out_hbm),
+    )):
+        outs.append(pltpu.make_async_copy(src, dst, out_sem.at[i + 1]))
+        outs[-1].start()
+    over_y().wait_recv()
     pass_copy(0).start()
-    update(1)
-    fifteen(1, grecv.at[1])
+    put(0, c).start()
+    pass_copy(0).wait_recv()
+    put(0, oc).start()
+    arrived(1, grecv.at[1])
     pass_copy(1).start()
+    put(1, c).start()
 
     pltpu.make_async_copy(hidp, hidp, hsend).wait()
     send_back.wait_send()
@@ -335,35 +417,40 @@
         def _():
             pltpu.make_async_copy(a2a.at[p], a2a.at[p], asend.at[p]).wait()
 
-        fifteen(p, gsend.at[p])
-        pass_copy(p).wait()
-    pltpu.make_async_copy(wg, w_hbm, w_sem).wait()
-    last = pltpu.make_async_copy(cg, cg_hbm, cg_sem)
-    last.start()
-    last.wait()
-
-
-def exchange(hidden, key_grad, cosine, sines, codes, scales, master, moment, second):
+        arrived(p, gsend.at[p])
+        pass_copy(p).wait_send()
+    over_y().wait_send()
+    pltpu.make_async_copy(hg, hg_hbm, hg_sem).wait()
+    for out in outs:
+        out.wait()
+    pass_copy(1).wait_recv()
+    put(1, oc).start()
+    pltpu.make_async_copy(cg, cg_hbm, cg_sem).wait()
+
+
+def exchange(hidden, key_grad, positions, frequency, codes, scales, master, moment, second):
     vmem = pl.BlockSpec(memory_space=pltpu.VMEM)
     anywhere = pl.BlockSpec(memory_space=pl.ANY)
+    hbm = pl.BlockSpec(memory_space=pltpu.HBM)
     dma = pltpu.SemaphoreType.DMA
     state = jax.ShapeDtypeStruct((32, 512), F32)
     return pl.pallas_call(
         exchange_kernel,
         out_shape=(
-            jax.ShapeDtypeStruct((8, 1024, 512), BF16),
-            jax.ShapeDtypeStruct((256, 512), BF16),
+            jax.ShapeDtypeStruct((256, 8192), BF16),
             jax.ShapeDtypeStruct((256, 512), BF16),
             state, state, state, state,
             jax.ShapeDtypeStruct((8, 2, 2, 32, 640), BF16),
         ),
-        in_specs=[anywhere] + [vmem] * 8,
-        out_specs=(anywhere,) + (vmem,) * 6 + (anywhere,),
+        in_specs=[hbm] * 2 + [vmem] * 2 + [hbm, vmem] + [hbm] * 3,
+        out_specs=(anywhere,) * 7,
         scratch_shapes=[
             pltpu.VMEM((256, 8192), BF16),
             pltpu.VMEM((4, 256, 1024), BF16),
             pltpu.VMEM((256, 512), BF16),
+            pltpu.VMEM((256, 512), BF16),
             pltpu.VMEM((8, 1024, 512), BF16),
+            pltpu.VMEM((256, 8192), BF16),
             pltpu.VMEM((2, 4, 128, 256), F32),
             pltpu.VMEM((2, 4, STEPS, 128, 256), BF16),
             pltpu.VMEM((2, 4, STEPS, 128, 256), BF16),
@@ -371,44 +458,49 @@
             pltpu.VMEM((2, 16, 32, 256), BF16),
             pltpu.VMEM((8, 2, 2, 32, 640), BF16),
             pltpu.VMEM((256, 512), F32),
-            dma, dma, dma,
+            pltpu.VMEM((256, 512), BF16),
+            pltpu.VMEM((1024, 512), BF16),
+            pltpu.VMEM((256, 512), BF16),
+            pltpu.VMEM((7, 32, 512), F32),
+            dma((6,)), dma, dma, dma((5,)),
             dma, dma((4,)), dma, dma, dma, dma((8, 2, 2)),
-            dma, dma((2, 4, STEPS)),
-            dma((2,)), dma((2,)), dma((2,)), dma((2,)), dma((2,)), dma((2,)),
+            dma, dma((2, 4, 2, STEPS)),
+            dma((2,)), dma((2,)), dma((2,)), dma((2,)), dma, dma, dma((2,)), dma((2,)),
         ],
         compiler_params=pltpu.CompilerParams(
-            has_side_effects=True, vmem_limit_bytes=60 * 1024 * 1024
+            collective_id=0, has_side_effects=True, vmem_limit_bytes=40 * 1024 * 1024
         ),
-    )(hidden, key_grad, cosine, sines, codes, scales, master, moment, second)
+    )(hidden, key_grad, positions, frequency, codes, scales, master, moment, second)
 
 
 def finish_kernel(
-    w, back, keys, grad, master, moment, second, cg,
-    hidden_grad, keys_out, grad_out, master_out, moment_out, second_out, codes_out, scales_out,
+    hg, keys, grad, master, moment, second, cg,
+    hg_out, keys_out, grad_out, master_out, moment_out, second_out, codes_out, scales_out,
+    spread, scales_v, in_sem, out_sem,
 ):
-    hidden_grad[...] = lax.dot_general(
-        back[...], w[0], (((1,), (1,)), ((), ())), preferred_element_type=F32
-    ).astype(BF16)
-
-    @pl.when(pl.program_id(0) == 0)
-    def _():
-        keys_out[...] = keys[...]
-        grad_out[...] = grad[...]
-        master_out[...] = master[...]
-        moment_out[...] = moment[...]
-        second_out[...] = second[...]
-        codes_out[...] = cg[:, 0:512]
-        scales_out[...] = cg[:, 512:640].astype(F32).T[0:2, :].astype(BF16)
-
-
-def finish(w, back, keys, grad, master, moment, second, cg):
-    def whole(*shape):
-        return pl.BlockSpec(shape, lambda i: (0,) * len(shape))
-
+    load = pltpu.make_async_copy(cg.at[:, pl.ds(512, 128)], spread, in_sem)
+    load.start()
+    pairs = (
+        (hg, hg_out), (cg.at[:, pl.ds(0, 512)], codes_out), (keys, keys_out), (grad, grad_out),
+        (master, master_out), (moment, moment_out), (second, second_out),
+    )
+    stores = [pltpu.make_async_copy(a, b, out_sem.at[i]) for i, (a, b) in enumerate(pairs)]
+    for store in stores:
+        store.start()
+    load.wait()
+    scales_v[...] = spread[...].astype(F32).T[0:2, :].astype(BF16)
+    stores.append(pltpu.make_async_copy(scales_v, scales_out, out_sem.at[7]))
+    stores[-1].start()
+    for store in stores:
+        store.wait()
+
+
+def finish(hg, keys, grad, master, moment, second, cg):
+    anywhere = pl.BlockSpec(memory_space=pl.ANY)
+    hbm = pl.BlockSpec(memory_space=pltpu.HBM)
     state = jax.ShapeDtypeStruct((32, 512), F32)
     return pl.pallas_call(
         finish_kernel,
-        grid=(8,),
         out_shape=(
             jax.ShapeDtypeStruct((256, 8192), BF16),
             jax.ShapeDtypeStruct((256, 512), BF16),
@@ -416,37 +508,29 @@
             jax.ShapeDtypeStruct((1024, 512), BF16),
             jax.ShapeDtypeStruct((2, 1024), BF16),
         ),
-        in_specs=[
-            pl.BlockSpec((1, 1024, 512), lambda i: (i, 0, 0)),
-            whole(256, 512), whole(256, 512),
-            whole(32, 512), whole(32, 512), whole(32, 512), whole(32, 512),
-            whole(1024, 640),
+        in_specs=[anywhere] * 7,
+        out_specs=(hbm,) * 8,
+        scratch_shapes=[
+            pltpu.VMEM((1024, 128), BF16), pltpu.VMEM((2, 1024), BF16),
+            pltpu.SemaphoreType.DMA, pltpu.SemaphoreType.DMA((8,)),
         ],
-        out_specs=(
-            pl.BlockSpec((256, 1024), lambda i: (0, i)),
-            whole(256, 512),
-            whole(32, 512), whole(32, 512), whole(32, 512), whole(32, 512),
-            whole(1024, 512), whole(2, 1024),
-        ),
-    )(w, back, keys, grad, master, moment, second, cg)
-
-
-def rotation(positions):
-    half_size = HEAD // 2
-    powers = jnp.arange(half_size, dtype=F32) * (-2.0 / HEAD)
-    frequency = jnp.power(F32(ROPE_BASE), powers)
-    both = jnp.concatenate([frequency, frequency])
-    angles = positions.astype(F32)[:, None] * both[None, :]
-    return jnp.cos(angles), jnp.sin(angles)
+        compiler_params=pltpu.CompilerParams(vmem_limit_bytes=4 * 1024 * 1024),
+    )(hg, keys, grad, master, moment, second, cg)
 
 
 def shards(hidden, key_grad, positions, weight_codes, weight_scales, master, moment, second):
-    cosine, sines = rotation(positions)
-    w, back, keys, grad, master_out, moment_out, second_out, cg = exchange(
-        hidden, key_grad, cosine, sines, weight_codes, weight_scales.T, master, moment, second
+    hidden, key_grad, weight_codes, master, moment, second = (
+        pltpu.with_memory_space_constraint(v, pltpu.HBM)
+        for v in (hidden, key_grad, weight_codes, master, moment, second)
+    )
+    half = jnp.arange(HEAD // 2, dtype=F32) * (-2.0 / HEAD)
+    frequency = jnp.power(F32(ROPE_BASE), jnp.concatenate([half, half]))[None, :]
+    hg, keys, grad, master_out, moment_out, second_out, cg = exchange(
+        hidden, key_grad, positions.reshape(2, 128), frequency, weight_codes, weight_scales.T,
+        master, moment, second,
     )
     hidden_grad, keys, grad, master_out, moment_out, second_out, codes, scales = finish(
-        w, back, keys, grad, master_out, moment_out, second_out, cg.reshape(1024, 640)
+        hg, keys, grad, master_out, moment_out, second_out, cg.reshape(1024, 640)
     )
     return (keys, hidden_grad, grad, master_out, moment_out, second_out, codes, scales.T)
 

time: 114 us -> 91.1 us (0.80); the launches traced: 112 us -> 91 us
  Pallas kernels: 109 us -> 88.9 us
  other arithmetic: 2.01 us -> 0.09 us
  local copies, waits for them, and re-layouts: 0 us -> 1.37 us
    pallas_call x2, Pallas kernels: 109 us -> 88.9 us  [the longest x1 86.3 us: exchange(): pl.pallas_call(exchange_kernel, out_shape=(jax.ShapeDtypeStruct((256, 819...]
    unnamed x0 -> x4, local copies, waits for them, and re-layouts: none -> 1.37 us
    sin x1 -> x0, other arithmetic: 1.24 us -> none  [rotation(): return (jnp.cos(angles), jnp.sin(angles))]
where the time goes in v2:
time: 91.1 us; the launch traced here: 91 us
  Pallas kernels  88.9 us (98%)
  local copies, waits for them, and re-layouts  1.37 us (2%)
    pallas_call x1, Pallas kernels, exchange(): pl.pallas_call(exchange_kernel, out_shape=(jax.ShapeDtypeStruct((256, 819...  86.3 us
    pallas_call x1, Pallas kernels, finish(): pl.pallas_call(finish_kernel, out_shape=(jax.ShapeDtypeStruct((256, 8192)...  2.59 us

profile of v2, /device:TPU:71, one launch (start us, length us, event | category | flops | bytes accessed | tf_op | source)
XLA Modules:
  0.0 91.0 jit_solution(8218924112557818574)
XLA Ops:
  0.6 0.1 maximum_power_fusion.frequency
  0.7 0.0 copy-start
  0.7 0.7 copy-done
  1.4 0.0 copy-start.1
  1.4 0.7 copy-done.1
  2.1 86.3 %shard_map.143 = (bf16[256,8192]{1,0:T(8,128)(2,1)S(1)}, bf16[256,512]{1,0:T(8,128)(2,1)S(1)}, f32[32,512]{1,0:T(8,128)S(1)}, f32[32,512]{1,0:T(8,128)S(1)}, f32...) custom-call(bf16[256,8192]{1,0:T(8,128)(2,1)} %hid_hbm.1, ...), custom_call_target="tpu_custom_call" | custom-call | tf_op jit(solution)/shard_map/pallas_call | solution.py:437
  88.4 2.6 %shard_map.144 = (bf16[256,8192]{1,0:T(8,128)(2,1)}, bf16[256,512]{1,0:T(8,128)(2,1)}, f32[32,512]{1,0:T(8,128)}, f32[32,512]{1,0:T(8,128)}, f32[32,512]{1,0:T(8...) custom-call(bf16[256,8192]{1,0:T(8,128)(2,1)S(1)} %get-tuple-element.23.hg, ...), custom_call_target="tpu_custom_call" | custom-call | tf_op jit(solution)/shard_map/pallas_call | solution.py:502
  (1 shorter events, 0.0 us)
Async XLA Ops:
  0.7 0.7 copy-start
  1.4 0.7 copy-start.1

commit v3 on v2

v3 whole, which is shorter than its diff:
```python
import jax
import jax.numpy as jnp
from jax import lax
from jax.experimental import pallas as pl
from jax.experimental.pallas import tpu as pltpu
from jax.sharding import PartitionSpec as P

HEAD = 128
ROPE_BASE = 1000000.0
LEARN_RATE = 0.002
FIRST_DECAY = 0.9
SECOND_DECAY = 0.95
FIRST_FIX = 0.9999734386011124
SECOND_FIX = 0.994079470779666
ADAM_EPSILON = 1e-08
SCALE_EPSILON = 1e-06
CODE_RANGE = 127.0

MESH = pl.DeviceIdType.MESH
F32 = jnp.float32
BF16 = jnp.bfloat16
ZN = 8
STEPS = ZN - 1
WIDTH = (256, 128)
LAG = 2


def device(z, y, x, core):
    return (z * 4 + lax.div(y, 2) * 2 + core, x * 2 + lax.rem(y, 2))


def dot_rows(a, b):
    return lax.dot_general(a, b, (((0,), (0,)), ((), ())), preferred_element_type=F32)


def exchange_kernel(
    hid_hbm, key_grad_hbm, positions_hbm, frequency, codes_hbm, scales_hbm, master_hbm, moment_hbm,
    second_hbm,
    hg_hbm, keys_hbm, grad_hbm, master_out_hbm, moment_out_hbm, second_out_hbm, cg_hbm, sc_hbm,
    hid, hidp, back_out, backp, wg, hg, pbuf, sendbuf, recvbuf, zsum, a2a, cg, acc,
    key_grad, codes, keys_out, state, positions, scales, bpart, b1, b2src, b2, sc, acc0,
    in_sem, hg_sem, cg_sem, out_sem, hsend, hfirst, hrest, bsend, brecv, wsend, wrecv,
    zsend, zrecv, zrecv1, asend, arecv, gsend, grecv, b1send, b1recv, b2send, b2recv, ssend, srecv, s2send, s2recv, ysend, yrecv, dsend, drecv,
):
    master, moment, second, grad_out, master_out, moment_out, second_out = (
        state.at[i] for i in range(7)
    )
    wide = lax.axis_index("wide")
    narrow = lax.axis_index("narrow")
    z, yh, c = lax.div(wide, 4), lax.rem(lax.div(wide, 2), 2), lax.rem(wide, 2)
    x, yl = lax.div(narrow, 2), lax.rem(narrow, 2)
    y = yh * 2 + yl
    oc = 1 - c
    partner = device(z, y, x, oc)
    xs = {d: lax.rem(x + d + 4, 4) for d in (-1, 1, 2)}
    xs[0] = x
    ys = {d: lax.rem(y + d + 4, 4) for d in (-1, 1)}

    loads = [
        pltpu.make_async_copy(src, dst, in_sem.at[i])
        for i, (src, dst) in enumerate((
            (positions_hbm, positions), (key_grad_hbm, key_grad), (hid_hbm, hid),
            (scales_hbm, scales), (codes_hbm, codes),
            (master_hbm, master), (moment_hbm, moment), (second_hbm, second),
        ))
    ]
    for load in loads:
        load.start()

    barrier = pltpu.get_barrier_semaphore()

    @pl.loop(0, 32)
    def _(i):
        to = device(z, lax.rem(lax.div(i, 2), 4), lax.div(i, 8), lax.rem(i, 2))

        @pl.when((to[0] != wide) | (to[1] != narrow))
        def _():
            pl.semaphore_signal(barrier, inc=1, device_id=to, device_id_type=MESH)

    @pl.loop(0, 16)
    def _(i):
        @pl.when(lax.div(i, 2) != z)
        def _():
            to = device(lax.div(i, 2), lax.rem(i, 2) * 2 + yl, x, c)
            pl.semaphore_signal(barrier, inc=1, device_id=to, device_id_type=MESH)

    def way_of(xd):
        return 1 if xd < 2 else -1

    def send_hidden(xd, i):
        at = lax.rem(z + way_of(xd) * (i - 1) + 2 * ZN, ZN)
        src = pl.ds(pl.multiple_of((xd * 2 + oc) * 1024 + at * 128, 128), 128)
        dst = pl.ds(pl.multiple_of(at * 128, 128), 128)
        sem = hfirst.at[xd] if isinstance(i, int) else hrest.at[xd]
        return pltpu.make_async_remote_copy(
            hid.at[:, src], hidp.at[xd, :, dst], hsend, sem, partner, MESH
        )

    loads[0].wait()
    place = jnp.concatenate(
        [jnp.broadcast_to(positions[i : i + 1, :].astype(F32), (128, 128)).T for i in range(2)], 0
    )
    angle = place * frequency[...]
    cos = jnp.cos(angle)
    sin = jnp.sin(angle)
    lane = lax.broadcasted_iota(jnp.int32, (256, HEAD), 1)
    sin = jnp.where(lane < HEAD // 2, -sin, sin)
    loads[1].wait()
    for h in range(4):
        s = slice(h * HEAD, (h + 1) * HEAD)
        v = key_grad[:, s].astype(F32)
        back_out[:, s] = (v * cos - pltpu.roll(v, HEAD // 2, 1) * sin).astype(BF16)
    send_back = pltpu.make_async_remote_copy(back_out, backp, bsend, brecv, partner, MESH)

    def chunk(xb, lo, half, q):
        return wg.at[xb * 2 + lo, pl.ds(pl.multiple_of(half * 512 + q * 256, 256), 256)]

    def w_copy(xb, lo, half, q, target):
        ref = chunk(xb, lo, half, q)
        sem = wrecv.at[xb * 2 + lo, half, q]
        return pltpu.make_async_remote_copy(ref, ref, wsend, sem, target, MESH)

    def w_wait(xb, lo, half, q):
        w_copy(xb, lo, half, q, partner).wait_recv()

    def to_x(xb, q, d):
        w_copy(xb, yl, c, q, device(z, y, xs[d], c)).start()

    def to_y(xb, q):
        w_copy(xb, yl, c, q, device(z, ys[1 - 2 * q], x, c)).start()

    def to_partner(xb, lo, q):
        w_copy(xb, lo, c, q, partner).start()

    pl.semaphore_wait(barrier, 45)
    loads[2].wait()
    for xd in range(4):
        send_hidden(xd, 0).start()
    send_back.start()

    @pl.loop(1, ZN)
    def _(i):
        for xd in range(4):
            send_hidden(xd, i).start()

    pick = (
        lax.broadcasted_iota(jnp.int32, (2, 512), 1) // 256
        == lax.broadcasted_iota(jnp.int32, (2, 512), 0)
    ).astype(BF16)

    loads[3].wait()
    loads[4].wait()

    @pl.loop(0, 8)
    def _(i):
        rows = pl.ds(pl.multiple_of(i * 128, 128), 128)
        factor = dot_rows(scales[:, rows], pick)
        wg[narrow, rows, :] = (codes[rows, :].astype(F32) * factor).astype(BF16)
    for q in range(2):
        to_x(x, q, 1)
        to_x(x, q, -1)
        to_y(x, q)

    def hg_copy(block):
        cols = pl.ds(pl.multiple_of(block * 1024, 1024), 1024)
        return pltpu.make_async_copy(hg.at[:, cols], hg_hbm.at[:, cols], hg_sem)

    def use_block(xb, lo, first=False):
        block = xb * 2 + lo
        if first:
            acc[...] = jnp.zeros_like(acc)
        else:
            w_wait(xb, lo, oc, 0)
            w_wait(xb, lo, oc, 1)

        @pl.loop(0, 4)
        def _(i):
            cols = pl.ds(pl.multiple_of(block * 1024 + i * 256, 256), 256)
            w = wg[block, pl.ds(pl.multiple_of(i * 256, 256), 256), :]
            acc[...] += jnp.dot(hid[:, cols], w, preferred_element_type=F32)
            hg[:, cols] = lax.dot_general(
                back_out[...], w, (((1,), (1,)), ((), ())), preferred_element_type=F32
            ).astype(BF16)

        hg_copy(block).start()

    def partial(xd, at, cols):
        own = pl.ds(pl.multiple_of((xd * 2 + c) * 1024 + at * 128, 128), 128)
        other = pl.ds(pl.multiple_of(at * 128, 128), 128)
        return dot_rows(hid[:, own], back_out[:, cols]) + dot_rows(
            hidp[xd, :, other], backp[:, cols]
        )

    def partials(p, step):
        for xd in range(4):
            at = lax.rem(z - way_of(xd) * (step + 1) + 2 * ZN, ZN)
            cols = slice(p * 256, p * 256 + WIDTH[p])
            pbuf[p, xd, :, 0 : WIDTH[p]] = partial(xd, at, cols)

    def part_rows(p, half):
        return slice(half * 64, half * 64 + 64) if p == 0 else slice(0, 128)

    def z_copy(p, xd, half, step):
        to = device(lax.rem(z + way_of(xd) + ZN, ZN), y, x, c)
        rows, cols = part_rows(p, half), slice(0, WIDTH[p])
        sem = zrecv.at[xd, half, step] if p == 0 else zrecv1.at[xd, step]
        return pltpu.make_async_remote_copy(
            sendbuf.at[p, xd, step, rows, cols], recvbuf.at[p, xd, step, rows, cols],
            zsend.at[p], sem, to, MESH,
        )

    def z_step(p, step):
        cols = slice(0, WIDTH[p])
        for half in range(2 - p):
            rows = part_rows(p, half)
            for xd in (0, 2, 1, 3):
                @pl.when(step > 0)
                def _():
                    z_copy(p, xd, half, step - 1).wait_recv()
                    pbuf[p, xd, rows, cols] += recvbuf[p, xd, step - 1, rows, cols].astype(F32)

                sendbuf[p, xd, step, rows, cols] = pbuf[p, xd, rows, cols].astype(BF16)
                z_copy(p, xd, half, step).start()
        if p == 0:
            @pl.when(step == 0)
            def _():
                for xd in range(4):
                    rest = hidp.at[xd, :, 0 : 7 * 128]
                    pltpu.make_async_copy(rest, rest, hrest.at[xd]).wait()

        partials(p, step + 1)

    def target(i):
        xd, yhd, cd = lax.div(i, 4), lax.rem(lax.div(i, 2), 2), lax.rem(i, 2)
        mine = (xd == x) & (yl == c) & (yhd == yh) & (cd == c)
        rows = pl.ds(pl.multiple_of(yhd * 64 + cd * 32, 32), 32)
        return xd, rows, mine, device(z, yhd * 2 + c, xd, cd)

    def send_plane(i, source, dst, send, recv):
        xd, rows, mine, to = target(i)
        src = source(xd, rows)

        @pl.when(mine)
        def _():
            pltpu.make_async_copy(src, dst, recv).start()

        @pl.when(jnp.logical_not(mine))
        def _():
            pltpu.make_async_remote_copy(src, dst, send, recv, to, MESH).start()

    def sent_plane(ref, send):
        @pl.when(yl == c)
        def _():
            part = ref.at[pl.ds(0, 15)]
            pltpu.make_async_copy(part, part, send).wait()

        @pl.when(yl != c)
        def _():
            pltpu.make_async_copy(ref, ref, send).wait()

    def to_plane(p):
        cols = slice(0, WIDTH[p])
        for xd in range(4):
            for half in range(2 - p):
                z_copy(p, xd, half, STEPS - 1).wait_recv()
            zsum[p, xd, :, cols] = (
                pbuf[p, xd, :, cols] + recvbuf[p, xd, STEPS - 1, :, cols].astype(F32)
            ).astype(BF16)

        @pl.loop(0, 16)
        def _(i):
            send_plane(
                i, lambda xd, rows: zsum.at[p, xd, rows, cols],
                a2a.at[p, x * 4 + y, :, cols], asend.at[p], arecv.at[p],
            )

    def plane_first(xd):
        for k in range(2):
            own = pl.ds(pl.multiple_of((xd * 2 + c) * 1024 + k * 512, 512), 512)
            other = slice(k * 512, k * 512 + 512)
            term = dot_rows(hid[:, own], back_out[:, 384:512]) + dot_rows(
                hidp[xd, :, other], backp[:, 384:512]
            )
            bpart[xd, k * 4 : k * 4 + 4] = term.astype(BF16).reshape(4, 128, 128)

        @pl.loop(xd * 4, xd * 4 + 4)
        def _(i):
            send_plane(
                i, lambda xd, rows: bpart.at[xd, :, rows], b1.at[x * 4 + y], b1send, b1recv
            )

    def then_z(i):
        return pltpu.make_async_remote_copy(
            b2src.at[i], b2.at[z], b2send, b2recv, device(i, y, x, c), MESH
        )

    def plane_done():
        pltpu.make_async_copy(b1, b1, b1recv).wait()

        @pl.loop(0, ZN)
        def _(i):
            total = b1[0, i].astype(F32)
            for k in range(1, 16):
                total = total + b1[k, i].astype(F32)
            b2src[i] = total.astype(BF16)

            @pl.when(i != z)
            def _():
                then_z(i).start()

        b2[z] = b2src[z]

    def span(p):
        return slice(p * 256, p * 256 + 256)

    def code_copy(p, i):
        zd, yhd = lax.div(i, 2), lax.rem(i, 2)
        ref = cg.at[z, yh, c, :, span(p)]
        mine = (zd == z) & (yhd == yh)
        skip = mine if p == 1 else mine | (yhd != yh)
        return skip, pltpu.make_async_remote_copy(
            ref, ref, gsend.at[p], grecv.at[p], device(zd, yhd * 2 + yl, x, c), MESH
        )

    def scale_copy(i):
        ref = sc.at[z, yh, c]
        to = device(lax.div(i, 2), lax.rem(i, 2) * 2 + yl, x, c)
        return pltpu.make_async_remote_copy(ref, ref, ssend, srecv, to, MESH)

    def over_y():
        ref = cg.at[:, yh, c, :, span(0)]
        to = device(z, (1 - yh) * 2 + yl, x, c)
        return pltpu.make_async_remote_copy(ref, ref, ysend, yrecv, to, MESH)

    def update(p):
        came = a2a.at[p, :, :, 0 : WIDTH[p]]
        pltpu.make_async_copy(came, came, arecv.at[p]).wait()
        total = a2a[p, 0, :, 0 : WIDTH[p]].astype(F32)
        for i in range(1, 16):
            total = total + a2a[p, i, :, 0 : WIDTH[p]].astype(F32)
        if p == 1:
            most = b2.at[pl.ds(0, 7)]
            pltpu.make_async_copy(most, most, b2recv).wait()
            rest = b2[0].astype(F32)
            for i in range(1, ZN):
                rest = rest + b2[i].astype(F32)
            total = jnp.concatenate([total, rest], 1)
        cols = slice(p * 256, (p + 1) * 256)
        gradient = total / 256.0
        moment_new = FIRST_DECAY * moment[:, cols] + (1.0 - FIRST_DECAY) * gradient
        second_new = SECOND_DECAY * second[:, cols] + (1.0 - SECOND_DECAY) * gradient * gradient
        step_size = moment_new / FIRST_FIX / (jnp.sqrt(second_new / SECOND_FIX) + ADAM_EPSILON)
        master_new = master[:, cols] - LEARN_RATE * step_size
        grad_out[:, cols] = gradient
        moment_out[:, cols] = moment_new
        second_out[:, cols] = second_new
        master_out[:, cols] = master_new
        peak = jnp.max(jnp.abs(master_new), axis=1, keepdims=True)
        scale = ((peak + SCALE_EPSILON) / CODE_RANGE).astype(BF16).astype(F32)
        cg[z, yh, c, :, cols] = (master_new / scale).astype(BF16)
        spread = jnp.broadcast_to(scale, (32, HEAD))
        if p == 0:
            acc0[...] = spread
        else:
            at = lax.broadcasted_iota(jnp.int32, (32, HEAD), 1)
            spread = jnp.where(at == 0, acc0[...], spread)
            turned = jnp.concatenate([spread] * 4, 0).T
            group = lax.broadcasted_iota(jnp.int32, (16, HEAD), 1) // 32
            sc[z, yh, c] = jnp.where(group == yh * 2 + c, turned[0:16], 0.0).astype(BF16)

        @pl.loop(0, 16)
        def _(i):
            skip, remote = code_copy(p, i)

            @pl.when(jnp.logical_not(skip))
            def _():
                remote.start()
                if p == 1:
                    scale_copy(i).start()

    def arrived(p, sem):
        same = cg.at[pl.ds(0, 7), 0, 0, :, span(0)] if p == 0 else a2a.at[0, pl.ds(0, 15)]
        pltpu.make_async_copy(same, same, sem).wait()

    def scales_arrived(sem):
        same = b1.at[0:15, 0, 0:16]
        pltpu.make_async_copy(same, same, sem).wait()

    def pass_scales():
        ref = sc.at[:, :, c]
        return pltpu.make_async_remote_copy(ref, ref, s2send, s2recv, partner, MESH)

    def put(p, core):
        ref = cg.at[:, :, core, :, span(p)]
        return pltpu.make_async_copy(ref, cg_hbm.at[:, :, core, :, span(p)], cg_sem)

    def pass_copy(p):
        ref = cg.at[:, :, c, :, span(p)]
        return pltpu.make_async_remote_copy(
            ref, ref, dsend.at[p], drecv.at[p], partner, MESH
        )

    for xd in range(4):
        send_hidden(xd, 0).wait_recv()
    send_back.wait_recv()
    partials(0, 0)

    @pl.loop(0, STEPS + LAG)
    def _(t):
        @pl.when(t < STEPS)
        def _():
            z_step(0, t)

        @pl.when(t == LAG - 1)
        def _():
            partials(1, 0)

        @pl.when(t >= LAG)
        def _():
            z_step(1, t - LAG)

        for k in range(4):
            @pl.when(t == k)
            def _():
                plane_first(k)

        @pl.when(t == 2)
        def _():
            w_wait(xs[-1], yl, c, 0)
            to_x(xs[-1], 0, 1)
            to_y(xs[-1], 0)
            to_partner(xs[-1], yl, 0)
            w_wait(xs[1], yl, c, 0)
            to_y(xs[1], 0)
            to_partner(xs[1], yl, 0)
            for q in range(2):
                w_wait(x, 1 - yl, c, q)
                to_partner(x, 1 - yl, q)
            use_block(x, yl, True)

        @pl.when(t == 4)
        def _():
            w_wait(xs[1], yl, c, 1)
            to_x(xs[1], 1, -1)
            to_y(xs[1], 1)
            to_partner(xs[1], yl, 1)
            w_wait(xs[-1], yl, c, 1)
            to_y(xs[-1], 1)
            to_partner(xs[-1], yl, 1)
            use_block(x, 1 - yl)

        @pl.when(t == 5)
        def _():
            for d in (-1, 1):
                use_block(xs[d], yl)

        @pl.when(t == 7)
        def _():
            to_plane(0)
            plane_done()

        @pl.when(t == 8)
        def _():
            for q in range(2):
                w_wait(xs[2], yl, c, q)
                to_y(xs[2], q)
                to_partner(xs[2], yl, q)

    to_plane(1)
    for load in loads[5:]:
        load.wait()
    for d in (-1, 1):
        w_wait(xs[d], 1 - yl, c, 0)
        to_partner(xs[d], 1 - yl, 0)
    use_block(xs[2], yl)
    update(0)
    for d in (-1, 1):
        w_wait(xs[d], 1 - yl, c, 1)
        to_partner(xs[d], 1 - yl, 1)
    for d in (-1, 1):
        use_block(xs[d], 1 - yl)
    update(1)
    arrived(0, grecv.at[0])
    over_y().start()
    outs = []
    for i, (src, dst) in enumerate((
        (grad_out, grad_hbm), (master_out, master_out_hbm),
        (moment_out, moment_out_hbm), (second_out, second_out_hbm),
    )):
        outs.append(pltpu.make_async_copy(src, dst, out_sem.at[i + 1]))
        outs[-1].start()
    for q in range(2):
        w_wait(xs[2], 1 - yl, c, q)
        to_partner(xs[2], 1 - yl, q)
    over_y().wait_recv()
    pass_copy(0).start()
    put(0, c).start()
    use_block(xs[2], 1 - yl)
    for h in range(4):
        s = slice(h * HEAD, (h + 1) * HEAD)
        v = acc[:, s]
        keys_out[:, s] = (v * cos + pltpu.roll(v, HEAD // 2, 1) * sin).astype(BF16)
    outs.append(pltpu.make_async_copy(keys_out, keys_hbm, out_sem.at[0]))
    outs[-1].start()
    pass_copy(0).wait_recv()
    put(0, oc).start()
    arrived(1, grecv.at[1])
    pass_copy(1).start()
    put(1, c).start()
    scales_arrived(srecv)
    pass_scales().start()

    pltpu.make_async_copy(hidp, hidp, hsend).wait()
    send_back.wait_send()
    pltpu.make_async_copy(wg.at[pl.ds(0, 7)], wg.at[pl.ds(0, 7)], wsend).wait()
    for p in range(2):
        sent = sendbuf.at[p, :, :, :, 0 : WIDTH[p]]
        pltpu.make_async_copy(sent, sent, zsend.at[p]).wait()
        sent_plane(a2a.at[p, :, :, 0 : WIDTH[p]], asend.at[p])
        arrived(p, gsend.at[p])
        pass_copy(p).wait_send()
    over_y().wait_send()
    sent_plane(b1, b1send)
    most = b2.at[pl.ds(0, 7)]
    pltpu.make_async_copy(most, most, b2send).wait()
    scales_arrived(ssend)
    pltpu.make_async_copy(hg, hg_hbm, hg_sem).wait()
    for out in outs:
        out.wait()
    pass_copy(1).wait_recv()
    put(1, oc).start()
    pass_scales().wait()
    last = pltpu.make_async_copy(sc, sc_hbm, out_sem.at[5])
    last.start()
    last.wait()
    pltpu.make_async_copy(cg, cg_hbm, cg_sem).wait()


def exchange(hidden, key_grad, positions, frequency, codes, scales, master, moment, second):
    vmem = pl.BlockSpec(memory_space=pltpu.VMEM)
    anywhere = pl.BlockSpec(memory_space=pl.ANY)
    hbm = pl.BlockSpec(memory_space=pltpu.HBM)
    dma = pltpu.SemaphoreType.DMA
    state = jax.ShapeDtypeStruct((32, 512), F32)
    return pl.pallas_call(
        exchange_kernel,
        out_shape=(
            jax.ShapeDtypeStruct((256, 8192), BF16),
            jax.ShapeDtypeStruct((256, 512), BF16),
            state, state, state, state,
            jax.ShapeDtypeStruct((8, 2, 2, 32, 512), BF16),
            jax.ShapeDtypeStruct((8, 2, 2, 16, 128), BF16),
        ),
        in_specs=[hbm] * 3 + [vmem] + [hbm] * 5,
        out_specs=(anywhere,) * 8,
        scratch_shapes=[
            pltpu.VMEM((256, 8192), BF16),
            pltpu.VMEM((4, 256, 1024), BF16),
            pltpu.VMEM((256, 512), BF16),
            pltpu.VMEM((256, 512), BF16),
            pltpu.VMEM((8, 1024, 512), BF16),
            pltpu.VMEM((256, 8192), BF16),
            pltpu.VMEM((2, 4, 128, 256), F32),
            pltpu.VMEM((2, 4, STEPS, 128, 256), BF16),
            pltpu.VMEM((2, 4, STEPS, 128, 256), BF16),
            pltpu.VMEM((2, 4, 128, 256), BF16),
            pltpu.VMEM((2, 16, 32, 256), BF16),
            pltpu.VMEM((8, 2, 2, 32, 512), BF16),
            pltpu.VMEM((256, 512), F32),
            pltpu.VMEM((256, 512), BF16),
            pltpu.VMEM((1024, 512), BF16),
            pltpu.VMEM((256, 512), BF16),
            pltpu.VMEM((7, 32, 512), F32),
            pltpu.VMEM((2, 128), jnp.int32),
            pltpu.VMEM((2, 1024), BF16),
            pltpu.VMEM((4, 8, 128, 128), BF16),
            pltpu.VMEM((16, 8, 32, 128), BF16),
            pltpu.VMEM((8, 32, 128), BF16),
            pltpu.VMEM((8, 32, 128), BF16),
            pltpu.VMEM((8, 2, 2, 16, 128), BF16),
            pltpu.VMEM((32, 128), F32),
            dma((8,)), dma, dma, dma((6,)),
            dma, dma((4,)), dma((4,)), dma, dma, dma, dma((8, 2, 2)),
            dma((2,)), dma((4, 2, STEPS)), dma((4, STEPS)),
            dma((2,)), dma((2,)), dma((2,)), dma((2,)),
            dma, dma, dma, dma, dma, dma, dma, dma,
            dma, dma, dma((2,)), dma((2,)),
        ],
        compiler_params=pltpu.CompilerParams(
            collective_id=0, has_side_effects=True, vmem_limit_bytes=44 * 1024 * 1024
        ),
    )(hidden, key_grad, positions, frequency, codes, scales, master, moment, second)


def finish_kernel(
    hg, keys, grad, master, moment, second, cg, sc,
    hg_out, keys_out, grad_out, master_out, moment_out, second_out, codes_out, scales_out,
    spread, scales_v, in_sem, out_sem,
):
    load = pltpu.make_async_copy(sc, spread, in_sem)
    load.start()
    pairs = (
        *((hg.at[pl.ds(64 * i, 64)], hg_out.at[pl.ds(64 * i, 64)]) for i in range(4)),
        (cg, codes_out), (keys, keys_out), (grad, grad_out),
        (master, master_out), (moment, moment_out), (second, second_out),
    )
    stores = [pltpu.make_async_copy(a, b, out_sem.at[i]) for i, (a, b) in enumerate(pairs)]
    for store in stores:
        store.start()
    load.wait()
    for i in range(8):
        total = spread[4 * i].astype(F32)
        for k in range(1, 4):
            total = total + spread[4 * i + k].astype(F32)
        scales_v[:, i * 128 : (i + 1) * 128] = total[0:2, :].astype(BF16)
    stores.append(pltpu.make_async_copy(scales_v, scales_out, out_sem.at[10]))
    stores[-1].start()
    for store in stores:
        store.wait()


def finish(hg, keys, grad, master, moment, second, cg, sc):
    anywhere = pl.BlockSpec(memory_space=pl.ANY)
    hbm = pl.BlockSpec(memory_space=pltpu.HBM)
    state = jax.ShapeDtypeStruct((32, 512), F32)
    return pl.pallas_call(
        finish_kernel,
        out_shape=(
            jax.ShapeDtypeStruct((256, 8192), BF16),
            jax.ShapeDtypeStruct((256, 512), BF16),
            state, state, state, state,
            jax.ShapeDtypeStruct((1024, 512), BF16),
            jax.ShapeDtypeStruct((2, 1024), BF16),
        ),
        in_specs=[anywhere] * 8,
        out_specs=(hbm,) * 8,
        scratch_shapes=[
            pltpu.VMEM((32, 16, 128), BF16), pltpu.VMEM((2, 1024), BF16),
            pltpu.SemaphoreType.DMA, pltpu.SemaphoreType.DMA((11,)),
        ],
        compiler_params=pltpu.CompilerParams(vmem_limit_bytes=4 * 1024 * 1024),
    )(hg, keys, grad, master, moment, second, cg, sc)


def shards(hidden, key_grad, positions, weight_codes, weight_scales, master, moment, second):
    positions, weight_scales = positions.reshape(2, 128), weight_scales.T
    hidden, key_grad, positions, weight_codes, weight_scales, master, moment, second = (
        pltpu.with_memory_space_constraint(v, pltpu.HBM)
        for v in (
            hidden, key_grad, positions, weight_codes, weight_scales, master, moment, second
        )
    )
    half = jnp.arange(HEAD // 2, dtype=F32) * (-2.0 / HEAD)
    frequency = jnp.power(F32(ROPE_BASE), jnp.concatenate([half, half]))[None, :]
    hg, keys, grad, master_out, moment_out, second_out, cg, sc = exchange(
        hidden, key_grad, positions, frequency, weight_codes, weight_scales,
        master, moment, second,
    )
    hidden_grad, keys, grad, master_out, moment_out, second_out, codes, scales = finish(
        hg, keys, grad, master_out, moment_out, second_out, cg.reshape(1024, 512),
        sc.reshape(32, 16, 128),
    )
    return (keys, hidden_grad, grad, master_out, moment_out, second_out, codes, scales.T)


def solution(mesh):
    in_specs = (
        P(("wide", "narrow"), None),
        P(("wide", "narrow"), None),
        P(("wide", "narrow")),
        P("narrow", None),
        P("narrow", None),
        P(("narrow", "wide"), None),
        P(("narrow", "wide"), None),
        P(("narrow", "wide"), None),
    )
    out_specs = (
        P(("wide", "narrow"), None),
        P(("wide", "narrow"), None),
        P(("narrow", "wide"), None),
        P(("narrow", "wide"), None),
        P(("narrow", "wide"), None),
        P(("narrow", "wide"), None),
        P("narrow", None),
        P("narrow", None),
    )
    return jax.shard_map(shards, mesh=mesh, in_specs=in_specs, out_specs=out_specs, check_vma=False)
```

time: 91.1 us -> 78.2 us (0.86); the launches traced: 91 us -> 76.9 us
  Pallas kernels: 88.9 us -> 76.2 us
  local copies, waits for them, and re-layouts: 1.37 us -> 0 us
    pallas_call x1, Pallas kernels: 86.3 us -> 73.4 us  [exchange(): pl.pallas_call(exchange_kernel, out_shape=(jax.ShapeDtypeStruct((256, 819...]
    unnamed x4 -> x0, local copies, waits for them, and re-layouts: 1.37 us -> none
where the time goes in v3:
time: 78.2 us; the launch traced here: 76.9 us
  Pallas kernels  76.2 us (97%)
    pallas_call x1, Pallas kernels, exchange(): pl.pallas_call(exchange_kernel, out_shape=(jax.ShapeDtypeStruct((256, 819...  73.4 us
    pallas_call x1, Pallas kernels, finish(): pl.pallas_call(finish_kernel, out_shape=(jax.ShapeDtypeStruct((256, 8192)...  2.74 us

profile of v3, /device:TPU:71, one launch (start us, length us, event | category | flops | bytes accessed | tf_op | source)
XLA Modules:
  0.0 76.9 jit_solution(15742581706049117832)
XLA Ops:
  0.6 0.1 maximum_power_fusion.frequency
  0.7 73.4 %shard_map.143 = (bf16[256,8192]{1,0:T(8,128)(2,1)S(1)}, bf16[256,512]{1,0:T(8,128)(2,1)S(1)}, f32[32,512]{1,0:T(8,128)S(1)}, f32[32,512]{1,0:T(8,128)S(1)}, f32...) custom-call(bf16[256,8192]{1,0:T(8,128)(2,1)} %hid_hbm.1, ...), custom_call_target="tpu_custom_call" | custom-call | tf_op jit(solution)/shard_map/pallas_call | solution.py:545
  74.2 2.7 %shard_map.144 = (bf16[256,8192]{1,0:T(8,128)(2,1)}, bf16[256,512]{1,0:T(8,128)(2,1)}, f32[32,512]{1,0:T(8,128)}, f32[32,512]{1,0:T(8,128)}, f32[32,512]{1,0:T(8...) custom-call(bf16[256,8192]{1,0:T(8,128)(2,1)S(1)} %get-tuple-element.24.hg, ...), custom_call_target="tpu_custom_call" | custom-call | tf_op jit(solution)/shard_map/pallas_call | solution.py:626
  (1 shorter events, 0.0 us)

commit v4 on v3

--- a/solution.py
+++ b/solution.py
@@ -472,13 +472,10 @@
     for d in (-1, 1):
         w_wait(xs[d], 1 - yl, c, 0)
         to_partner(xs[d], 1 - yl, 0)
-    use_block(xs[2], yl)
     update(0)
     for d in (-1, 1):
         w_wait(xs[d], 1 - yl, c, 1)
         to_partner(xs[d], 1 - yl, 1)
-    for d in (-1, 1):
-        use_block(xs[d], 1 - yl)
     update(1)
     arrived(0, grecv.at[0])
     over_y().start()
@@ -489,6 +486,9 @@
     )):
         outs.append(pltpu.make_async_copy(src, dst, out_sem.at[i + 1]))
         outs[-1].start()
+    use_block(xs[2], yl)
+    for d in (-1, 1):
+        use_block(xs[d], 1 - yl)
     for q in range(2):
         w_wait(xs[2], 1 - yl, c, q)
         to_partner(xs[2], 1 - yl, q)

time: 78.2 us -> 78.2 us (level)
  no operation moved by 1% of the time
where the time goes in v4:
time: 78.2 us; the launch traced here: 76.7 us
  Pallas kernels  76 us (97%)
    pallas_call x1, Pallas kernels, exchange(): pl.pallas_call(exchange_kernel, out_shape=(jax.ShapeDtypeStruct((256, 819...  73.3 us
    pallas_call x1, Pallas kernels, finish(): pl.pallas_call(finish_kernel, out_shape=(jax.ShapeDtypeStruct((256, 8192)...  2.74 us

profile of v4, /device:TPU:71, one launch (start us, length us, event | category | flops | bytes accessed | tf_op | source)
XLA Modules:
  0.0 76.7 jit_solution(1099164049266937658)
XLA Ops:
  0.6 0.1 maximum_power_fusion.frequency
  0.7 73.3 %shard_map.143 = (bf16[256,8192]{1,0:T(8,128)(2,1)S(1)}, bf16[256,512]{1,0:T(8,128)(2,1)S(1)}, f32[32,512]{1,0:T(8,128)S(1)}, f32[32,512]{1,0:T(8,128)S(1)}, f32...) custom-call(bf16[256,8192]{1,0:T(8,128)(2,1)} %hid_hbm.1, ...), custom_call_target="tpu_custom_call" | custom-call | tf_op jit(solution)/shard_map/pallas_call | solution.py:545
  74.0 2.7 %shard_map.144 = (bf16[256,8192]{1,0:T(8,128)(2,1)}, bf16[256,512]{1,0:T(8,128)(2,1)}, f32[32,512]{1,0:T(8,128)}, f32[32,512]{1,0:T(8,128)}, f32[32,512]{1,0:T(8...) custom-call(bf16[256,8192]{1,0:T(8,128)(2,1)S(1)} %get-tuple-element.24.hg, ...), custom_call_target="tpu_custom_call" | custom-call | tf_op jit(solution)/shard_map/pallas_call | solution.py:626
  (1 shorter events, 0.0 us)
